TPU v7x, 32 devices: a whole 2x2x4 slice. The times are simulated.
32 devices in a mesh: gx: 4 (over y, core), gy: 8 (over z, x).
Axes of the slice: x: 2, y: 2, z: 4, core: 2. Of those that a mesh axis runs over, the one named last changes fastest.
Arguments:
- old_master: float32 [32, 128, 1536], P('gx', 'gy'), may hold values from -3 to 3
- old_first: float32 [32, 128, 1536], P('gx', 'gy'), may hold values from -3 to 3
- old_second: float32 [32, 128, 1536], P('gx', 'gy'), may hold values from 0.01 to 1
- new_grad: bfloat16 [32, 128, 1536], P(('gx', 'gy')), may hold values from -3072 to 3072
- counts: int32 [32, 32], P(None, ('gx', 'gy')), may hold values from 1 to 72, as said below
- old_owner: int32 [32], replicated, may hold values from 0 to 31, each once
- new_owner: int32 [32], replicated, may hold values from 0 to 31, each once
Outputs:
- new_master: float32 [32, 128, 1536], P(('gx', 'gy'))
- new_first: float32 [32, 128, 1536], P(('gx', 'gy'))
- new_second: float32 [32, 128, 1536], P(('gx', 'gy'))
Inputs may be any that keep to these rules, and one draw needn't show every extreme that they name: `old_owner`: every number of 0 to 31 appears once. `new_owner`: every number of 0 to 31 appears once. `counts`: every device routed at least one token to every expert.
All inputs are finite; a program needn't handle non-finite values.
Results may differ from a plain program's by a relative error of at most 0.0003.
Values sent between devices are 32-bit elements; how exact they have to be, the bound alone decides.
No kernel may reach another device: no remote copies, remote signals or barrier semaphores. Data moves between devices by JAX's collectives and lax.ppermute only.
A program may use at most 64 MiB of HBM per device.

v0:
```python
import jax
import jax.numpy as jnp
from jax import lax
from jax.sharding import PartitionSpec as P

first_correction = 1.0 - 0.9**10
second_correction = 1.0 - 0.999**10


def adam_step(master, first, second, grad, slot_count):
    scaled = grad.astype(jnp.float32) / slot_count
    new_first = 0.9 * first + 0.1 * scaled
    new_second = 0.999 * second + 0.001 * scaled * scaled
    step_dir = new_first / first_correction / (jnp.sqrt(new_second / second_correction) + 1e-08)
    new_master = master - 0.01 * (step_dir + 0.1 * master)
    return (new_master, new_first, new_second)


def reorder(block, groups_x, groups_y):
    total_rows = block.shape[1]
    piece = total_rows // (groups_x * groups_y)
    shaped = block.reshape(1, groups_x, groups_y, piece, block.shape[2])
    return shaped.transpose(0, 2, 1, 3, 4).reshape(1, total_rows, block.shape[2])


def body(old_master, old_first, old_second, new_grad, counts, old_owner, new_owner):
    experts = old_owner.shape[0]
    groups_x = lax.axis_size("gx")
    groups_y = lax.axis_size("gy")
    my_slot = lax.axis_index("gx") * groups_y + lax.axis_index("gy")
    slots = jnp.arange(experts, dtype=jnp.int32)
    onehot = new_owner[:, None] == slots[None, :]
    source = jnp.sum(jnp.where(onehot, old_owner[:, None], 0), axis=0)
    local_counts = counts[:, 0].astype(jnp.float32)
    by_rows = (
        lax.all_to_all(old_master, "gx", split_axis=1, concat_axis=0, tiled=True),
        lax.all_to_all(old_first, "gx", split_axis=1, concat_axis=0, tiled=True),
        lax.all_to_all(old_second, "gx", split_axis=1, concat_axis=0, tiled=True),
    )
    permuted = tuple((jnp.take(state, source, axis=0) for state in by_rows))
    landed = lax.all_to_all(permuted, ("gx", "gy"), split_axis=0, concat_axis=1, tiled=True)
    arrived = tuple((reorder(state, groups_x, groups_y) for state in landed))
    totals = lax.psum(local_counts, ("gx", "gy"))
    slot_count = jnp.sum(jnp.where(new_owner == my_slot, totals, jnp.float32(0.0)))
    return adam_step(arrived[0], arrived[1], arrived[2], new_grad, slot_count)


def solution(mesh):
    placed = (
        P("gx", "gy", None),
        P("gx", "gy", None),
        P("gx", "gy", None),
        P(("gx", "gy"), None, None),
        P(None, ("gx", "gy")),
        P(),
        P(),
    )
    return jax.shard_map(
        body,
        mesh=mesh,
        in_specs=placed,
        out_specs=(
            P(("gx", "gy"), None, None),
            P(("gx", "gy"), None, None),
            P(("gx", "gy"), None, None),
        ),
        check_vma=False,
    )
```

profile of v0, /device:TPU:0, one launch (start us, length us, event | category | flops | bytes accessed | tf_op | source)
XLA Modules:
  0.0 156.1 jit_solution(17211418162359433335)
XLA Ops:
  0.6 2.5 %copy.67 = f32[8,16,1536]{2,0,1:T(8,128)} copy(f32[8,16,1536]{2,1,0:T(8,128)} %param.9) | data formatting | bytes 1572864 | tf_op args[0]
  3.1 0.0 copy-start
  3.1 4.4 %all-to-all-start = ((f32[8,16,1536]{2,0,1:T(8,128)}), f32[8,16,1536]{2,0,1:T(8,128)S(1)}, u32[]{:S(2)}, u32[]{:S(2)}) async-start(f32[8,16,1536]{2,0,1:T(8,128)} %copy.67), calls=%async_computation | async-start | bytes 1572864 | tf_op jit(solution)/shard_map/all_to_all | solution.py:36
  7.5 0.0 copy-done
  7.5 1.3 copy.72
  8.8 0.0 copy-start.1
  8.8 10.3 %all-to-all-done = f32[8,16,1536]{2,0,1:T(8,128)S(1)} async-done(((f32[8,16,1536]{2,0,1:T(8,128)}), f32[8,16,1536]{2,0,1:T(8,128)S(1)}, u32[]{:S(2)}, u32[]{:S(2)}) %all-to-all-start) | async-done | bytes 786464 | tf_op jit(solution)/shard_map/all_to_all | solution.py:36
  19.1 3.5 %all-to-all-start.2 = ((f32[8,16,1536]{2,0,1:T(8,128)}), f32[8,16,1536]{2,0,1:T(8,128)S(1)}, u32[]{:S(2)}, u32[]{:S(2)}) async-start(f32[8,16,1536]{2,0,1:T(8,128)} %copy.72), calls=%async_computation.2 | async-start | bytes 1572864 | tf_op jit(solution)/shard_map/all_to_all | solution.py:37
  22.6 0.0 copy-done.1
  22.6 1.3 copy.78
  24.0 0.0 copy-start.3
  24.0 0.0 copy-start.4
  24.0 10.2 %all-to-all-done.2 = f32[8,16,1536]{2,0,1:T(8,128)S(1)} async-done(((f32[8,16,1536]{2,0,1:T(8,128)}), f32[8,16,1536]{2,0,1:T(8,128)S(1)}, u32[]{:S(2)}, u32[]{:S(2)}) %all-to-all-start.2) | async-done | bytes 786464 | tf_op jit(solution)/shard_map/all_to_all | solution.py:37
  34.2 3.5 %all-to-all-start.4 = ((f32[8,16,1536]{2,0,1:T(8,128)}), f32[8,16,1536]{2,0,1:T(8,128)S(1)}, u32[]{:S(2)}, u32[]{:S(2)}) async-start(f32[8,16,1536]{2,0,1:T(8,128)} %copy.78), calls=%async_computation.4 | async-start | bytes 1572864 | tf_op jit(solution)/shard_map/all_to_all | solution.py:38
  37.7 0.0 copy-done.3
  37.7 0.0 copy-done.4
  37.7 0.1 select_reduce_fusion
  37.9 0.1 copy.104
  37.9 0.5 copy.69
  38.4 0.1 copy.102
  38.5 1.4 copy.74
  39.9 1.0 gather_fusion
  40.9 2.2 %gather_fusion.1 = f32[32,4,1536]{2,1,0:T(4,128)S(1)} fusion(f32[32,4,1536]{2,1,0:T(4,128)} %copy.74, s32[1024]{0:T(1024)S(1)} %pad_clamp_fusion), kind=kCustom, calls=%fused_computation.1.clone | custom fusion | bytes 1572992 | tf_op jit(solution)/shard_map/jit(_take)/gather | solution.py:40
  43.1 6.2 %all-to-all-done.4 = f32[8,16,1536]{2,0,1:T(8,128)S(1)} async-done(((f32[8,16,1536]{2,0,1:T(8,128)}), f32[8,16,1536]{2,0,1:T(8,128)S(1)}, u32[]{:S(2)}, u32[]{:S(2)}) %all-to-all-start.4) | async-done | bytes 786464 | tf_op jit(solution)/shard_map/all_to_all | solution.py:38
  49.3 0.1 copy.101
  49.4 0.5 copy.80
  49.9 1.0 gather_fusion.2
  50.9 1.5 broadcast_select_fusion
  52.4 27.2 %all_to_all.81 = f32[32,4,1536]{2,1,0:T(4,128)S(1)} all-to-all(f32[32,4,1536]{2,1,0:T(4,128)S(1)} %get-tuple-element.13), channel_id=1, replica_groups=mesh['gx'=4,'gy'=8] {'gx','gy'}, dimensions={0} | all-to-all | bytes 1572864 | tf_op jit(solution)/shard_map/all_to_all | solution.py:41
  79.6 24.0 %all_to_all.82 = f32[32,4,1536]{2,1,0:T(4,128)S(1)} all-to-all(f32[32,4,1536]{2,1,0:T(4,128)S(1)} %get-tuple-element.14), channel_id=1, replica_groups=mesh['gx'=4,'gy'=8] {'gx','gy'}, dimensions={0} | all-to-all | bytes 1572864 | tf_op jit(solution)/shard_map/all_to_all | solution.py:41
  103.6 0.0 copy-start.5
  103.6 2.8 %all-to-all-start.1 = ((f32[32,4,1536]{2,1,0:T(4,128)}), f32[32,4,1536]{2,1,0:T(4,128)S(1)}, u32[]{:S(2)}, u32[]{:S(2)}) async-start(f32[32,4,1536]{2,1,0:T(4,128)} %get-tuple-element.15), calls=%async_computation.1 | async-start | bytes 1572864 | tf_op jit(solution)/shard_map/all_to_all | solution.py:41
  106.4 0.0 copy-done.5
  106.4 43.1 %psum.7 = f32[32]{0:T(128)S(1)} all-reduce(f32[32]{0:T(128)S(1)} %convert_bitcast_fusion), channel_id=1, replica_groups=mesh['gx'=4,'gy'=8] {'gx','gy'}, use_global_device_ids=true, to_apply=%region_1.3 | all-reduce | flops 32 | bytes 256 | tf_op jit(solution)/shard_map/psum | solution.py:43
  149.5 0.7 fusion.3
  150.2 0.3 fusion.1
  150.5 0.8 copy.82
  151.3 0.3 fusion.2
  151.6 0.8 copy.76
  152.4 0.0 all-to-all-done.1
  152.4 0.3 copy.103
  152.7 0.0 copy-start.2
  152.7 0.8 copy.71
  153.5 0.2 copy-done.2
  153.7 2.5 %multiply_subtract_fusion = (f32[1,128,1536]{2,1,0:T(8,128)}, f32[1,128,1536]{2,1,0:T(8,128)}, f32[1,128,1536]{2,1,0:T(8,128)}) fusion(f32[1,128,1536]{2,0,1:T(1,128)S(1)} %bitcast.45, f32[]{:T(128)} %fusion.3, bf16[1,128,1536]{2,1,0:T(8,128)(2,1)S(1)} %copy-done.2, f32[1,128,1536]{2,0,1:T(1,128)S(1)} %bitcast.44, f32[1,128,1536]{2,0,1:T(1,128)S(1)} %bitcast.43), kind=kLoop, calls=%fused_computation.14 | loop fusion | flops 2949120 | bytes 5111812 | tf_op jit(solution)/shard_map/sub | solution.py:15
  (4 shorter events, 0.0 us)
Async XLA Ops:
  3.1 4.4 %copy-start = (f32[8,16,1536]{2,1,0:T(8,128)S(1)}, f32[8,16,1536]{2,1,0:T(8,128)}, u32[]{:S(2)}) copy-start(f32[8,16,1536]{2,1,0:T(8,128)} %param.10) | copy-start | bytes 2359300
  3.1 16.0 %all-to-all-start = ((f32[8,16,1536]{2,0,1:T(8,128)}), f32[8,16,1536]{2,0,1:T(8,128)S(1)}, u32[]{:S(2)}, u32[]{:S(2)}) async-start(f32[8,16,1536]{2,0,1:T(8,128)} %copy.67), calls=%async_computation | async-start | bytes 1572864 | tf_op jit(solution)/shard_map/all_to_all | solution.py:36
  8.8 13.8 %copy-start.1 = (f32[8,16,1536]{2,1,0:T(8,128)S(1)}, f32[8,16,1536]{2,1,0:T(8,128)}, u32[]{:S(2)}) copy-start(f32[8,16,1536]{2,1,0:T(8,128)} %param.11) | copy-start | bytes 2359300
  19.1 15.1 %all-to-all-start.2 = ((f32[8,16,1536]{2,0,1:T(8,128)}), f32[8,16,1536]{2,0,1:T(8,128)S(1)}, u32[]{:S(2)}, u32[]{:S(2)}) async-start(f32[8,16,1536]{2,0,1:T(8,128)} %copy.72), calls=%async_computation.2 | async-start | bytes 1572864 | tf_op jit(solution)/shard_map/all_to_all | solution.py:37
  24.0 13.7 %copy-start.3 = (s32[32]{0:T(128)S(1)}, s32[32]{0:T(128)}, u32[]{:S(2)}) copy-start(s32[32]{0:T(128)} %param.15) | copy-start | bytes 388
  24.0 13.8 %copy-start.4 = (s32[32]{0:T(128)S(1)}, s32[32]{0:T(128)}, u32[]{:S(2)}) copy-start(s32[32]{0:T(128)} %param.14) | copy-start | bytes 388
  34.2 15.1 %all-to-all-start.4 = ((f32[8,16,1536]{2,0,1:T(8,128)}), f32[8,16,1536]{2,0,1:T(8,128)S(1)}, u32[]{:S(2)}, u32[]{:S(2)}) async-start(f32[8,16,1536]{2,0,1:T(8,128)} %copy.78), calls=%async_computation.4 | async-start | bytes 1572864 | tf_op jit(solution)/shard_map/all_to_all | solution.py:38
  103.6 2.8 %copy-start.5 = (s32[32,1]{0,1:T(1,128)S(1)}, s32[32,1]{0,1:T(1,128)}, u32[]{:S(2)}) copy-start(s32[32,1]{0,1:T(1,128)} %param.13) | copy-start | bytes 388
  103.6 48.8 %all-to-all-start.1 = ((f32[32,4,1536]{2,1,0:T(4,128)}), f32[32,4,1536]{2,1,0:T(4,128)S(1)}, u32[]{:S(2)}, u32[]{:S(2)}) async-start(f32[32,4,1536]{2,1,0:T(4,128)} %get-tuple-element.15), calls=%async_computation.1 | async-start | bytes 1572864 | tf_op jit(solution)/shard_map/all_to_all | solution.py:41
  152.7 1.0 copy-start.2
where the time goes:
time: 157 us; the launch traced here: 156 us
  blocking collectives  94.3 us (60%)
  waiting for transfers between devices  26.7 us (17%)
  local copies, waits for them, and re-layouts  14.8 us (9%)
  starting transfers between devices  14.1 us (9%)
  other arithmetic  5.31 us (3%)
    all_to_all x2, blocking collectives, body(): lax.all_to_all(permuted, ('gx', 'gy'), split_axis=0, concat_axis=1, tiled...  51.2 us
    psum x1, blocking collectives, body(): totals = lax.psum(local_counts, ('gx', 'gy'))  43.1 us
    all_to_all x1, waiting for transfers between devices, body(): lax.all_to_all(old_master, 'gx', split_axis=1, concat_axis=0, tiled=True)  10.3 us
    all_to_all x1, waiting for transfers between devices, body(): lax.all_to_all(old_first, 'gx', split_axis=1, concat_axis=0, tiled=True)  10.2 us
    all_to_all x1, waiting for transfers between devices, body(): lax.all_to_all(old_second, 'gx', split_axis=1, concat_axis=0, tiled=True)  6.23 us
    unnamed x15, local copies, waits for them, and re-layouts  5.34 us
    all_to_all x1, starting transfers between devices, body(): lax.all_to_all(old_master, 'gx', split_axis=1, concat_axis=0, tiled=True)  4.4 us
    gather x3, local copies, waits for them, and re-layouts, body(): permuted = tuple((jnp.take(state, source, axis=0) for state in by_rows))  4.19 us
  transfers between devices with their start and end apart: 4, of which 3 were waited for; matrix products, arithmetic and copies ran while one was open for 7% of the time, Pallas kernels for 0%

commit v1 on v0

v1 whole, which is shorter than its diff:
```python
import jax
import jax.numpy as jnp
from jax import lax
from jax.experimental import pallas as pl
from jax.experimental.pallas import tpu as pltpu
from jax.sharding import PartitionSpec as P


first_correction = 1.0 - 0.9**10
second_correction = 1.0 - 0.999**10


def partner(index, step, size):
    if size & (size - 1) == 0:
        return index ^ step
    return (step - index) % size


def adam_kernel(place_ref, count_ref, grad_ref, piece_ref, *refs):
    master_out, first_out, second_out = refs[-3:]
    slot_count = count_ref[0]
    master = piece_ref[0]
    first = piece_ref[1]
    second = piece_ref[2]
    scaled = grad_ref[0].astype(jnp.float32) / slot_count
    new_first = 0.9 * first + 0.1 * scaled
    new_second = 0.999 * second + 0.001 * scaled * scaled
    step_dir = new_first / first_correction / (jnp.sqrt(new_second / second_correction) + 1e-08)
    master_out[0] = master - 0.01 * (step_dir + 0.1 * master)
    first_out[0] = new_first
    second_out[0] = new_second


def adam_chunk(place, slot_count, grad, piece, carried):
    _, rows, width = piece.shape
    out = jax.ShapeDtypeStruct(grad.shape, jnp.float32)
    spot = pl.BlockSpec((1, rows, width), lambda i, place_ref, count_ref: (0, place_ref[0], 0))
    whole = pl.BlockSpec((3, rows, width), lambda i, place_ref, count_ref: (0, 0, 0))
    apart = pl.BlockSpec(memory_space=pl.ANY)
    return pl.pallas_call(
        adam_kernel,
        grid_spec=pltpu.PrefetchScalarGridSpec(
            num_scalar_prefetch=2,
            grid=(1,),
            in_specs=[spot, whole] + [apart] * len(carried),
            out_specs=[spot] * 3,
        ),
        out_shape=[out] * 3,
        input_output_aliases={4 + j: j for j in range(len(carried))},
        compiler_params=pltpu.CompilerParams(vmem_limit_bytes=8 * 1024 * 1024),
    )(place, slot_count, grad, piece, *carried)


def body(order_k, old_master, old_first, old_second, new_grad, counts, old_owner, new_owner):
    groups_x = lax.axis_size("gx")
    groups_y = lax.axis_size("gy")
    held, _, _ = old_master.shape
    cores = 2 if groups_x % 2 == 0 else 1
    chips = groups_x // cores
    x = lax.axis_index("gx")
    y = lax.axis_index("gy")
    chip, core = x // cores, x % cores
    swap = [(i, (i // cores) * cores + (cores - 1 - i % cores)) for i in range(groups_x)]
    across = [
        [(i, ((i // cores + d) % chips) * cores + i % cores) for i in range(groups_x)]
        for d in range(1, chips)
    ]
    order = [jnp.int32(partner(y, k, groups_y)) for k in range(groups_y)]

    own = (old_master, old_first, old_second)
    if cores == 2:
        near = tuple(lax.ppermute(state, "gx", swap) for state in own)
    else:
        near = own

    columns = jnp.stack([((chip + d) % chips) * cores + core for d in range(chips)])
    slots = columns[:, None] * groups_y + jnp.stack(order)[None, :]
    onehot = new_owner[:, None, None] == slots[None]
    source = jnp.sum(jnp.where(onehot, old_owner[:, None, None], 0), axis=0)
    from_x, spot = source // held, source % held
    is_own = from_x % cores == core
    lag = (chip - from_x // cores + chips) % chips

    def held_piece(d, k):
        picked = [
            jnp.where(
                is_own[d, k],
                lax.dynamic_index_in_dim(a, spot[d, k], 0),
                lax.dynamic_index_in_dim(b, spot[d, k], 0),
            )
            for a, b in zip(own, near)
        ]
        return jnp.concatenate(picked, axis=0)

    tally = counts[:, 0].astype(jnp.float32)
    for pairs in across:
        tally = tally + lax.ppermute(counts[:, 0].astype(jnp.float32), "gx", pairs)
    if cores == 2:
        tally = tally + lax.ppermute(tally, "gx", swap)
    if groups_y & (groups_y - 1) == 0:
        step = 1
        while step < groups_y:
            tally = tally + lax.ppermute(tally, "gy", [(i, i ^ step) for i in range(groups_y)])
            step *= 2
    else:
        tally = lax.psum(tally, "gy")
    my_slot = x * groups_y + y
    slot_count = jnp.sum(jnp.where(new_owner == my_slot, tally, jnp.float32(0.0))).reshape(1)

    ready = {}
    for k in order_k:
        sent = []
        for d in range(1, chips):
            chosen = held_piece(d, k)
            sent.append(lax.ppermute(chosen, "gx", across[d - 1]))
        piece = held_piece(0, k)
        for d in range(1, chips):
            piece = jnp.where(lag[0, k] == d, sent[d - 1], piece)
        pairs = [(i, partner(i, k, groups_y)) for i in range(groups_y)]
        if any(a != b for a, b in pairs):
            piece = lax.ppermute(piece, "gy", pairs)
        ready[k] = piece

    carried = ()
    for k in order_k[-1:] + order_k[:-1]:
        carried = adam_chunk(order[k].reshape(1), slot_count, new_grad, ready[k], carried)
    return tuple(carried)


def solution(mesh):
    groups_y = mesh.shape["gy"]
    order_k = list(range(groups_y // 2, groups_y)) + list(range(groups_y // 2 - 1, -1, -1))

    def stepped(*args):
        return body(order_k, *args)

    placed = (
        P("gx", "gy", None),
        P("gx", "gy", None),
        P("gx", "gy", None),
        P(("gx", "gy"), None, None),
        P(None, ("gx", "gy")),
        P(),
        P(),
    )
    return jax.shard_map(
        stepped,
        mesh=mesh,
        in_specs=placed,
        out_specs=(
            P(("gx", "gy"), None, None),
            P(("gx", "gy"), None, None),
            P(("gx", "gy"), None, None),
        ),
        check_vma=False,
    )
```

time: 157 us -> 158 us (level)
  blocking collectives: 94.3 us -> 0 us
  between operations: 0.83 us -> 35.9 us
  other arithmetic: 5.31 us -> 33.9 us
  starting transfers between devices: 14.1 us -> 34.8 us
  waiting for transfers between devices: 26.7 us -> 37.9 us
  local copies, waits for them, and re-layouts: 14.8 us -> 3.85 us
  Pallas kernels: 0 us -> 10.8 us
    all_to_all x2 -> x0, blocking collectives: 51.2 us -> none  [body(): lax.all_to_all(permuted, ('gx', 'gy'), split_axis=0, concat_axis=1, tiled...]
    psum x1 -> x0, blocking collectives: 43.1 us -> none  [body(): totals = lax.psum(local_counts, ('gx', 'gy'))]
    ppermute x0 -> x23, waiting for transfers between devices: none -> 37.9 us  [the longest x7 18.8 us: body(): piece = lax.ppermute(piece, 'gy', pairs)]
    ppermute x0 -> x23, starting transfers between devices: none -> 34.8 us  [the longest x7 16.7 us: body(): piece = lax.ppermute(piece, 'gy', pairs)]
    select_n x2 -> x15, other arithmetic: 1.5 us -> 32.1 us  [the longest x6 31.7 us: held_piece(): jnp.where(is_own[d, k], lax.dynamic_index_in_dim(a, spot[d, k], 0), lax.d...]
    all_to_all x4 -> x0, waiting for transfers between devices: 26.7 us -> none  [the longest x1 10.3 us: body(): lax.all_to_all(old_master, 'gx', split_axis=1, concat_axis=0, tiled=True)]
    all_to_all x4 -> x0, starting transfers between devices: 14.1 us -> none  [the longest x1 4.4 us: body(): lax.all_to_all(old_master, 'gx', split_axis=1, concat_axis=0, tiled=True)]
    pallas_call x0 -> x8, Pallas kernels: none -> 10.8 us  [adam_chunk(): pl.pallas_call(adam_kernel, grid_spec=pltpu.PrefetchScalarGridSpec(num_sc...]
  transfers between devices with their start and end apart: 4 -> 23, of which waited for: 3 -> 10; matrix products, arithmetic and copies ran while one was open for 7% -> 19% of each run, Pallas kernels for 0% -> 6%
where the time goes in v1:
time: 158 us; the launch traced here: 157 us
  waiting for transfers between devices  37.9 us (24%)
  between operations  35.9 us (23%)
  starting transfers between devices  34.8 us (22%)
  other arithmetic  33.9 us (21%)
  Pallas kernels  10.8 us (7%)
  local copies, waits for them, and re-layouts  3.85 us (2%)
    select_n x6, other arithmetic, held_piece(): jnp.where(is_own[d, k], lax.dynamic_index_in_dim(a, spot[d, k], 0), lax.d...  31.7 us
    ppermute x7, waiting for transfers between devices, body(): piece = lax.ppermute(piece, 'gy', pairs)  18.8 us
    ppermute x8, waiting for transfers between devices, body(): sent.append(lax.ppermute(chosen, 'gx', across[d - 1]))  17 us
    ppermute x7, starting transfers between devices, body(): piece = lax.ppermute(piece, 'gy', pairs)  16.7 us
    pallas_call x8, Pallas kernels, adam_chunk(): pl.pallas_call(adam_kernel, grid_spec=pltpu.PrefetchScalarGridSpec(num_sc...  10.8 us
    ppermute x8, starting transfers between devices, body(): sent.append(lax.ppermute(chosen, 'gx', across[d - 1]))  8.33 us
    ppermute x3, starting transfers between devices, body(): lax.ppermute(tally, 'gy', [(i, i ^ step) for i in range(groups_y)])  5.72 us
  transfers between devices with their start and end apart: 23, of which 10 were waited for; matrix products, arithmetic and copies ran while one was open for 19% of the time, Pallas kernels for 6%

profile of v1, /device:TPU:0, one launch (start us, length us, event | category | flops | bytes accessed | tf_op | source)
XLA Modules:
  0.0 157.2 jit_solution(889828267910257185)
XLA Ops:
  0.6 0.7 convert_bitcast_fusion
  1.3 3.0 %collective-permute-start = (f32[32]{0:T(128)S(1)}, f32[32]{0:T(128)S(1)}, u32[]{:S(2)}, u32[]{:S(2)}) collective-permute-start(f32[32]{0:T(128)S(1)} %convert_bitcast_fusion), channel_id=1, source_target_pairs={{0,16},{8,24},{16,0},{24,8},{1,17},{9,25},{17,1},{25,9},{2,18},{10... | collective-permute-start | bytes 392 | tf_op jit(solution)/shard_map/ppermute | solution.py:97
  4.3 0.0 collective-permute-start.5
  4.3 0.5 collective-permute-start.6
  4.8 0.0 collective-permute-start.7
  4.8 0.1 add_multiply_fusion
  4.9 0.1 stack.44
  5.0 0.1 broadcast_add_fusion
  5.0 0.6 copy-done.4
  5.6 0.0 copy-done.5
  5.6 0.2 select_reduce_fusion
  5.9 0.7 fusion.5
  26.5 0.7 fusion.4
  36.0 0.7 fusion.6
  37.3 0.0 copy-start.6
  37.9 0.0 collective-permute-done
  37.9 0.1 copy-done.6
  38.0 0.5 collective-permute-start.1
  39.8 0.0 collective-permute-done.1
  39.8 1.6 collective-permute-start.2
  42.7 0.8 collective-permute-done.2
  43.5 1.6 %collective-permute-start.3 = (f32[32]{0:T(128)S(1)}, f32[32]{0:T(128)S(1)}, u32[]{:S(2)}, u32[]{:S(2)}) collective-permute-start(f32[32]{0:T(128)S(1)} %add.206), channel_id=1, source_target_pairs={{0,2},{1,3},{2,0},{3,1},{4,6},{5,7},{6,4},{7,5},{8,10},{9,11},{10,... | collective-permute-start | bytes 392 | tf_op jit(solution)/shard_map/ppermute | solution.py:103
  46.3 0.7 collective-permute-done.3
  47.1 2.6 %collective-permute-start.4 = (f32[32]{0:T(128)S(1)}, f32[32]{0:T(128)S(1)}, u32[]{:S(2)}, u32[]{:S(2)}) collective-permute-start(f32[32]{0:T(128)S(1)} %add.207), channel_id=1, source_target_pairs={{0,4},{1,5},{2,6},{3,7},{4,0},{5,1},{6,2},{7,3},{8,12},{9,13},{10,... | collective-permute-start | bytes 392 | tf_op jit(solution)/shard_map/ppermute | solution.py:103
  50.9 0.6 collective-permute-done.4
  51.5 0.6 fusion.2
  52.2 6.3 %dynamic-slice_select_fusion.2 = (f32[1,16,1536]{2,1,0:T(8,128)S(1)}, f32[1,16,1536]{2,1,0:T(8,128)S(1)}, f32[1,16,1536]{2,1,0:T(8,128)S(1)}, f32[1,16,1536]{2,1...) fusion(f32[8,16,1536]{2,1,0:T(8,128)S(1)} %collective-permute-d, ...), kind=kLoop, calls=%fused_computation.18 | loop fusion | flops 196608 | bytes 2359336 | tf_op jit(solution)/shard_map/jit(_where)/select_n | solution.py:86
  58.5 0.0 copy-start.3
  58.5 0.0 collective-permute-done.6
  58.5 5.1 %dynamic-slice_select_fusion.1 = (f32[1,16,1536]{2,1,0:T(8,128)S(1)}, f32[1,16,1536]{2,1,0:T(8,128)S(1)}, f32[1,16,1536]{2,1,0:T(8,128)S(1)}, f32[1,16,1536]{2,1...) fusion(f32[8,16,1536]{2,1,0:T(8,128)S(1)} %collective-permute-d, ...), kind=kLoop, calls=%fused_computation.17 | loop fusion | flops 196608 | bytes 2359336 | tf_op jit(solution)/shard_map/jit(_where)/select_n | solution.py:86
  63.7 5.0 %dynamic-slice_select_fusion = (f32[1,16,1536]{2,1,0:T(8,128)S(1)}, f32[1,16,1536]{2,1,0:T(8,128)S(1)}, f32[1,16,1536]{2,1,0:T(8,128)S(1)}, f32[1,16,1536]{2,1,0...) fusion(f32[8,16,1536]{2,1,0:T(8,128)S(1)} %collective-permute-d, ...), kind=kLoop, calls=%fused_computation.16 | loop fusion | flops 196608 | bytes 2359336 | tf_op jit(solution)/shard_map/jit(_where)/select_n | solution.py:86
  68.7 0.2 collective-permute-start.16
  69.0 1.9 %collective-permute-start.18 = (f32[3,16,1536]{2,1,0:T(8,128)S(1)}, f32[3,16,1536]{2,1,0:T(8,128)S(1)}, u32[]{:S(2)}, u32[]{:S(2)}) collective-permute-start(f32[3,16,1536]{2,1,0:T(8,128)S(1)} %pad_maximum_fusion.5), channel_id=1, source_target_pairs={{0,16},{8,24},{16,0},{24,8},{1,17},{9,25},{17,1},{25,9},{2,18},{10... | collective-permute-start | bytes 884744 | tf_op jit(solution)/shard_map/ppermute | solution.py:115
  70.9 0.2 collective-permute-start.20
  71.2 1.9 %collective-permute-start.22 = (f32[3,16,1536]{2,1,0:T(8,128)S(1)}, f32[3,16,1536]{2,1,0:T(8,128)S(1)}, u32[]{:S(2)}, u32[]{:S(2)}) collective-permute-start(f32[3,16,1536]{2,1,0:T(8,128)S(1)} %pad_maximum_fusion.7), channel_id=1, source_target_pairs={{0,16},{8,24},{16,0},{24,8},{1,17},{9,25},{17,1},{25,9},{2,18},{10... | collective-permute-start | bytes 884744 | tf_op jit(solution)/shard_map/ppermute | solution.py:115
  73.1 5.1 %dynamic-slice_select_fusion.26 = (f32[1,16,1536]{2,1,0:T(8,128)S(1)}, f32[1,16,1536]{2,1,0:T(8,128)S(1)}, f32[1,16,1536]{2,1,0:T(8,128)S(1)}, f32[1,16,1536]{2,...) fusion(f32[8,16,1536]{2,1,0:T(8,128)S(1)} %collective-permute-d, ...), kind=kLoop, calls=%fused_computation.42 | loop fusion | flops 196608 | bytes 2359336 | tf_op jit(solution)/shard_map/jit(_where)/select_n | solution.py:86
  78.2 5.1 %dynamic-slice_select_fusion.25 = (f32[1,16,1536]{2,1,0:T(8,128)S(1)}, f32[1,16,1536]{2,1,0:T(8,128)S(1)}, f32[1,16,1536]{2,1,0:T(8,128)S(1)}, f32[1,16,1536]{2,...) fusion(f32[8,16,1536]{2,1,0:T(8,128)S(1)} %collective-permute-d, ...), kind=kLoop, calls=%fused_computation.41 | loop fusion | flops 196608 | bytes 2359336 | tf_op jit(solution)/shard_map/jit(_where)/select_n | solution.py:86
  83.3 5.1 %dynamic-slice_select_fusion.24 = (f32[1,16,1536]{2,1,0:T(8,128)S(1)}, f32[1,16,1536]{2,1,0:T(8,128)S(1)}, f32[1,16,1536]{2,1,0:T(8,128)S(1)}, f32[1,16,1536]{2,...) fusion(f32[8,16,1536]{2,1,0:T(8,128)S(1)} %collective-permute-d, ...), kind=kLoop, calls=%fused_computation.40 | loop fusion | flops 196608 | bytes 2359336 | tf_op jit(solution)/shard_map/jit(_where)/select_n | solution.py:86
  88.4 0.2 collective-permute-start.8
  88.8 1.9 %collective-permute-start.10 = (f32[3,16,1536]{2,1,0:T(8,128)S(1)}, f32[3,16,1536]{2,1,0:T(8,128)S(1)}, u32[]{:S(2)}, u32[]{:S(2)}) collective-permute-start(f32[3,16,1536]{2,1,0:T(8,128)S(1)} %pad_maximum_fusion.1), channel_id=1, source_target_pairs={{0,16},{8,24},{16,0},{24,8},{1,17},{9,25},{17,1},{25,9},{2,18},{10... | collective-permute-start | bytes 884744 | tf_op jit(solution)/shard_map/ppermute | solution.py:115
  90.7 0.2 collective-permute-start.12
  91.0 0.3 collective-permute-done.20
  91.3 1.6 %collective-permute-start.14 = (f32[3,16,1536]{2,1,0:T(8,128)S(1)}, f32[3,16,1536]{2,1,0:T(8,128)S(1)}, u32[]{:S(2)}, u32[]{:S(2)}) collective-permute-start(f32[3,16,1536]{2,1,0:T(8,128)S(1)} %pad_maximum_fusion.3), channel_id=1, source_target_pairs={{0,16},{8,24},{16,0},{24,8},{1,17},{9,25},{17,1},{25,9},{2,18},{10... | collective-permute-start | bytes 884744 | tf_op jit(solution)/shard_map/ppermute | solution.py:115
  93.0 11.0 %collective-permute-done.8 = f32[3,16,1536]{2,1,0:T(8,128)S(1)} collective-permute-done((f32[3,16,1536]{2,1,0:T(8,128)S(1)}, f32[3,16,1536]{2,1,0:T(8,128)S(1)}, u32[]{:S(2)}, u32[]{:S(2)}) %collective-permute-start.8) | collective-permute-done | bytes 294944 | tf_op jit(solution)/shard_map/ppermute | solution.py:115
  104.0 3.6 %collective-permute-start.17 = (f32[3,16,1536]{2,1,0:T(8,128)S(1)}, f32[3,16,1536]{2,1,0:T(8,128)S(1)}, u32[]{:S(2)}, u32[]{:S(2)}) collective-permute-start(f32[3,16,1536]{2,1,0:T(8,128)S(1)} %maximum_select_fusion.4), channel_id=1, source_target_pairs={{0,6},{1,7},{2,4},{3,5},{4,2},{5,3},{6,0},{7,1},{8,14},{9,15},{10,... | collective-permute-start | bytes 884744 | tf_op jit(solution)/shard_map/ppermute | solution.py:121
  107.6 2.7 %collective-permute-done.10 = f32[3,16,1536]{2,1,0:T(8,128)S(1)} collective-permute-done((f32[3,16,1536]{2,1,0:T(8,128)S(1)}, f32[3,16,1536]{2,1,0:T(8,128)S(1)}, u32[]{:S(2)}, u32[]{:S(2)}) %collective-permute-start.10) | collective-permute-done | bytes 294944 | tf_op jit(solution)/shard_map/ppermute | solution.py:115
  110.3 3.5 %collective-permute-start.19 = (f32[3,16,1536]{2,1,0:T(8,128)S(1)}, f32[3,16,1536]{2,1,0:T(8,128)S(1)}, u32[]{:S(2)}, u32[]{:S(2)}) collective-permute-start(f32[3,16,1536]{2,1,0:T(8,128)S(1)} %maximum_select_fusion.5), channel_id=1, source_target_pairs={{0,5},{1,4},{2,7},{3,6},{4,1},{5,0},{6,3},{7,2},{8,13},{9,12},{10,... | collective-permute-start | bytes 884744 | tf_op jit(solution)/shard_map/ppermute | solution.py:121
  113.8 2.2 %collective-permute-done.12 = f32[3,16,1536]{2,1,0:T(8,128)S(1)} collective-permute-done((f32[3,16,1536]{2,1,0:T(8,128)S(1)}, f32[3,16,1536]{2,1,0:T(8,128)S(1)}, u32[]{:S(2)}, u32[]{:S(2)}) %collective-permute-start.12) | collective-permute-done | bytes 294944 | tf_op jit(solution)/shard_map/ppermute | solution.py:115
  116.0 2.3 %collective-permute-start.21 = (f32[3,16,1536]{2,1,0:T(8,128)S(1)}, f32[3,16,1536]{2,1,0:T(8,128)S(1)}, u32[]{:S(2)}, u32[]{:S(2)}) collective-permute-start(f32[3,16,1536]{2,1,0:T(8,128)S(1)} %maximum_select_fusion.6), channel_id=1, source_target_pairs={{0,4},{1,5},{2,6},{3,7},{4,0},{5,1},{6,2},{7,3},{8,12},{9,13},{10,... | collective-permute-start | bytes 884744 | tf_op jit(solution)/shard_map/ppermute | solution.py:121
  118.4 0.8 collective-permute-done.14
  119.2 1.3 collective-permute-start.9
  120.6 1.4 collective-permute-start.11
  122.0 13.9 %collective-permute-done.19.piece_ref = f32[3,16,1536]{2,1,0:T(8,128)S(1)} collective-permute-done((f32[3,16,1536]{2,1,0:T(8,128)S(1)}, f32[3,16,1536]{2,1,0:T(8,128)S(1)}, u32[]{:S(2)}, u32[]{:S(2)}) %collective-permute-start.19) | collective-permute-done | bytes 294944 | tf_op jit(solution)/shard_map/ppermute | solution.py:121
  135.9 4.9 %collective-permute-done.21.piece_ref = f32[3,16,1536]{2,1,0:T(8,128)S(1)} collective-permute-done((f32[3,16,1536]{2,1,0:T(8,128)S(1)}, f32[3,16,1536]{2,1,0:T(8,128)S(1)}, u32[]{:S(2)}, u32[]{:S(2)}) %collective-permute-start.21) | collective-permute-done | bytes 294944 | tf_op jit(solution)/shard_map/ppermute | solution.py:121
  140.8 4.6 %collective-permute-start.15 = (f32[3,16,1536]{2,1,0:T(8,128)S(1)}, f32[3,16,1536]{2,1,0:T(8,128)S(1)}, u32[]{:S(2)}, u32[]{:S(2)}) collective-permute-start(f32[3,16,1536]{2,1,0:T(8,128)S(1)} %maximum_select_fusion.3), channel_id=1, source_target_pairs={{0,7},{1,6},{2,5},{3,4},{4,3},{5,2},{6,1},{7,0},{8,15},{9,14},{10,... | collective-permute-start | bytes 884744 | tf_op jit(solution)/shard_map/ppermute | solution.py:121
  145.4 1.0 copy-done
  146.4 1.3 shard_map.94
  147.7 1.3 shard_map.95
  149.1 1.3 shard_map.96
  150.4 1.4 shard_map.97
  151.8 1.4 shard_map.98
  153.1 1.4 shard_map.99
  154.5 1.4 shard_map.100
  155.8 1.4 shard_map.101
  (41 shorter events, 0.6 us)
Async XLA Ops:
  1.3 36.6 %collective-permute-start = (f32[32]{0:T(128)S(1)}, f32[32]{0:T(128)S(1)}, u32[]{:S(2)}, u32[]{:S(2)}) collective-permute-start(f32[32]{0:T(128)S(1)} %convert_bitcast_fusion), channel_id=1, source_target_pairs={{0,16},{8,24},{16,0},{24,8},{1,17},{9,25},{17,1},{25,9},{2,18},{10... | collective-permute-start | bytes 392 | tf_op jit(solution)/shard_map/ppermute | solution.py:97
  4.3 47.9 %collective-permute-start.5 = (f32[8,16,1536]{2,1,0:T(8,128)}, f32[8,16,1536]{2,1,0:T(8,128)S(1)}, u32[]{:S(2)}, u32[]{:S(2)}) collective-permute-start(f32[8,16,1536]{2,1,0:T(8,128)} %param.7), channel_id=1, source_target_pairs={{0,8},{8,0},{16,24},{24,16},{1,9},{9,1},{17,25},{25,17},{2,10},{10... | collective-permute-start | bytes 2359304 | tf_op jit(solution)/shard_map/ppermute | solution.py:72
  4.3 54.2 %collective-permute-start.6 = (f32[8,16,1536]{2,1,0:T(8,128)}, f32[8,16,1536]{2,1,0:T(8,128)S(1)}, u32[]{:S(2)}, u32[]{:S(2)}) collective-permute-start(f32[8,16,1536]{2,1,0:T(8,128)} %param.8), channel_id=1, source_target_pairs={{0,8},{8,0},{16,24},{24,16},{1,9},{9,1},{17,25},{25,17},{2,10},{10... | collective-permute-start | bytes 2359304 | tf_op jit(solution)/shard_map/ppermute | solution.py:72
  4.8 58.8 %collective-permute-start.7 = (f32[8,16,1536]{2,1,0:T(8,128)}, f32[8,16,1536]{2,1,0:T(8,128)S(1)}, u32[]{:S(2)}, u32[]{:S(2)}) collective-permute-start(f32[8,16,1536]{2,1,0:T(8,128)} %param.9), channel_id=1, source_target_pairs={{0,8},{8,0},{16,24},{24,16},{1,9},{9,1},{17,25},{25,17},{2,10},{10... | collective-permute-start | bytes 2359304 | tf_op jit(solution)/shard_map/ppermute | solution.py:72
  5.0 0.7 copy-start.4
  5.0 0.7 copy-start.5
  37.3 0.7 copy-start.6
  38.0 1.8 %collective-permute-start.1 = (f32[32]{0:T(128)S(1)}, f32[32]{0:T(128)S(1)}, u32[]{:S(2)}, u32[]{:S(2)}) collective-permute-start(f32[32]{0:T(128)S(1)} %fusion.3), channel_id=1, source_target_pairs={{0,8},{8,0},{16,24},{24,16},{1,9},{9,1},{17,25},{25,17},{2,10},{10... | collective-permute-start | bytes 392 | tf_op jit(solution)/shard_map/ppermute | solution.py:99
  39.8 3.6 %collective-permute-start.2 = (f32[32]{0:T(128)S(1)}, f32[32]{0:T(128)S(1)}, u32[]{:S(2)}, u32[]{:S(2)}) collective-permute-start(f32[32]{0:T(128)S(1)} %add.205), channel_id=1, source_target_pairs={{0,1},{1,0},{2,3},{3,2},{4,5},{5,4},{6,7},{7,6},{8,9},{9,8},{10,11... | collective-permute-start | bytes 392 | tf_op jit(solution)/shard_map/ppermute | solution.py:103
  43.5 3.6 %collective-permute-start.3 = (f32[32]{0:T(128)S(1)}, f32[32]{0:T(128)S(1)}, u32[]{:S(2)}, u32[]{:S(2)}) collective-permute-start(f32[32]{0:T(128)S(1)} %add.206), channel_id=1, source_target_pairs={{0,2},{1,3},{2,0},{3,1},{4,6},{5,7},{6,4},{7,5},{8,10},{9,11},{10,... | collective-permute-start | bytes 392 | tf_op jit(solution)/shard_map/ppermute | solution.py:103
  47.1 4.5 %collective-permute-start.4 = (f32[32]{0:T(128)S(1)}, f32[32]{0:T(128)S(1)}, u32[]{:S(2)}, u32[]{:S(2)}) collective-permute-start(f32[32]{0:T(128)S(1)} %add.207), channel_id=1, source_target_pairs={{0,4},{1,5},{2,6},{3,7},{4,0},{5,1},{6,2},{7,3},{8,12},{9,13},{10,... | collective-permute-start | bytes 392 | tf_op jit(solution)/shard_map/ppermute | solution.py:103
  52.2 6.4 %copy-start.2 = (f32[8,16,1536]{2,1,0:T(8,128)S(1)}, f32[8,16,1536]{2,1,0:T(8,128)}, u32[]{:S(2)}) copy-start(f32[8,16,1536]{2,1,0:T(8,128)} %param.8) | copy-start | bytes 2359300
  58.5 5.2 %copy-start.3 = (f32[8,16,1536]{2,1,0:T(8,128)S(1)}, f32[8,16,1536]{2,1,0:T(8,128)}, u32[]{:S(2)}) copy-start(f32[8,16,1536]{2,1,0:T(8,128)} %param.9) | copy-start | bytes 2359300
  68.7 20.0 %collective-permute-start.16 = (f32[3,16,1536]{2,1,0:T(8,128)S(1)}, f32[3,16,1536]{2,1,0:T(8,128)S(1)}, u32[]{:S(2)}, u32[]{:S(2)}) collective-permute-start(f32[3,16,1536]{2,1,0:T(8,128)S(1)} %pad_maximum_fusion.4), channel_id=1, source_target_pairs={{0,16},{8,24},{16,0},{24,8},{1,17},{9,25},{17,1},{25,9},{2,18},{10... | collective-permute-start | bytes 884744 | tf_op jit(solution)/shard_map/ppermute | solution.py:115
  69.0 4.1 %copy-start.1 = (f32[8,16,1536]{2,1,0:T(8,128)S(1)}, f32[8,16,1536]{2,1,0:T(8,128)}, u32[]{:S(2)}) copy-start(f32[8,16,1536]{2,1,0:T(8,128)} %param.7) | copy-start | bytes 2359300
  69.0 21.7 %collective-permute-start.18 = (f32[3,16,1536]{2,1,0:T(8,128)S(1)}, f32[3,16,1536]{2,1,0:T(8,128)S(1)}, u32[]{:S(2)}, u32[]{:S(2)}) collective-permute-start(f32[3,16,1536]{2,1,0:T(8,128)S(1)} %pad_maximum_fusion.5), channel_id=1, source_target_pairs={{0,16},{8,24},{16,0},{24,8},{1,17},{9,25},{17,1},{25,9},{2,18},{10... | collective-permute-start | bytes 884744 | tf_op jit(solution)/shard_map/ppermute | solution.py:115
  70.9 20.4 %collective-permute-start.20 = (f32[3,16,1536]{2,1,0:T(8,128)S(1)}, f32[3,16,1536]{2,1,0:T(8,128)S(1)}, u32[]{:S(2)}, u32[]{:S(2)}) collective-permute-start(f32[3,16,1536]{2,1,0:T(8,128)S(1)} %pad_maximum_fusion.6), channel_id=1, source_target_pairs={{0,16},{8,24},{16,0},{24,8},{1,17},{9,25},{17,1},{25,9},{2,18},{10... | collective-permute-start | bytes 884744 | tf_op jit(solution)/shard_map/ppermute | solution.py:115
  71.2 49.4 %collective-permute-start.22 = (f32[3,16,1536]{2,1,0:T(8,128)S(1)}, f32[3,16,1536]{2,1,0:T(8,128)S(1)}, u32[]{:S(2)}, u32[]{:S(2)}) collective-permute-start(f32[3,16,1536]{2,1,0:T(8,128)S(1)} %pad_maximum_fusion.7), channel_id=1, source_target_pairs={{0,16},{8,24},{16,0},{24,8},{1,17},{9,25},{17,1},{25,9},{2,18},{10... | collective-permute-start | bytes 884744 | tf_op jit(solution)/shard_map/ppermute | solution.py:115
  88.4 15.5 %collective-permute-start.8 = (f32[3,16,1536]{2,1,0:T(8,128)S(1)}, f32[3,16,1536]{2,1,0:T(8,128)S(1)}, u32[]{:S(2)}, u32[]{:S(2)}) collective-permute-start(f32[3,16,1536]{2,1,0:T(8,128)S(1)} %pad_maximum_fusion), channel_id=1, source_target_pairs={{0,16},{8,24},{16,0},{24,8},{1,17},{9,25},{17,1},{25,9},{2,18},{10... | collective-permute-start | bytes 884744 | tf_op jit(solution)/shard_map/ppermute | solution.py:115
  88.8 21.5 %collective-permute-start.10 = (f32[3,16,1536]{2,1,0:T(8,128)S(1)}, f32[3,16,1536]{2,1,0:T(8,128)S(1)}, u32[]{:S(2)}, u32[]{:S(2)}) collective-permute-start(f32[3,16,1536]{2,1,0:T(8,128)S(1)} %pad_maximum_fusion.1), channel_id=1, source_target_pairs={{0,16},{8,24},{16,0},{24,8},{1,17},{9,25},{17,1},{25,9},{2,18},{10... | collective-permute-start | bytes 884744 | tf_op jit(solution)/shard_map/ppermute | solution.py:115
  90.7 25.3 %collective-permute-start.12 = (f32[3,16,1536]{2,1,0:T(8,128)S(1)}, f32[3,16,1536]{2,1,0:T(8,128)S(1)}, u32[]{:S(2)}, u32[]{:S(2)}) collective-permute-start(f32[3,16,1536]{2,1,0:T(8,128)S(1)} %pad_maximum_fusion.2), channel_id=1, source_target_pairs={{0,16},{8,24},{16,0},{24,8},{1,17},{9,25},{17,1},{25,9},{2,18},{10... | collective-permute-start | bytes 884744 | tf_op jit(solution)/shard_map/ppermute | solution.py:115
  91.3 27.9 %collective-permute-start.14 = (f32[3,16,1536]{2,1,0:T(8,128)S(1)}, f32[3,16,1536]{2,1,0:T(8,128)S(1)}, u32[]{:S(2)}, u32[]{:S(2)}) collective-permute-start(f32[3,16,1536]{2,1,0:T(8,128)S(1)} %pad_maximum_fusion.3), channel_id=1, source_target_pairs={{0,16},{8,24},{16,0},{24,8},{1,17},{9,25},{17,1},{25,9},{2,18},{10... | collective-permute-start | bytes 884744 | tf_op jit(solution)/shard_map/ppermute | solution.py:115
  104.0 46.5 %collective-permute-start.17 = (f32[3,16,1536]{2,1,0:T(8,128)S(1)}, f32[3,16,1536]{2,1,0:T(8,128)S(1)}, u32[]{:S(2)}, u32[]{:S(2)}) collective-permute-start(f32[3,16,1536]{2,1,0:T(8,128)S(1)} %maximum_select_fusion.4), channel_id=1, source_target_pairs={{0,6},{1,7},{2,4},{3,5},{4,2},{5,3},{6,0},{7,1},{8,14},{9,15},{10,... | collective-permute-start | bytes 884744 | tf_op jit(solution)/shard_map/ppermute | solution.py:121
  110.3 25.6 %collective-permute-start.19 = (f32[3,16,1536]{2,1,0:T(8,128)S(1)}, f32[3,16,1536]{2,1,0:T(8,128)S(1)}, u32[]{:S(2)}, u32[]{:S(2)}) collective-permute-start(f32[3,16,1536]{2,1,0:T(8,128)S(1)} %maximum_select_fusion.5), channel_id=1, source_target_pairs={{0,5},{1,4},{2,7},{3,6},{4,1},{5,0},{6,3},{7,2},{8,13},{9,12},{10,... | collective-permute-start | bytes 884744 | tf_op jit(solution)/shard_map/ppermute | solution.py:121
  116.0 24.7 %collective-permute-start.21 = (f32[3,16,1536]{2,1,0:T(8,128)S(1)}, f32[3,16,1536]{2,1,0:T(8,128)S(1)}, u32[]{:S(2)}, u32[]{:S(2)}) collective-permute-start(f32[3,16,1536]{2,1,0:T(8,128)S(1)} %maximum_select_fusion.6), channel_id=1, source_target_pairs={{0,4},{1,5},{2,6},{3,7},{4,0},{5,1},{6,2},{7,3},{8,12},{9,13},{10,... | collective-permute-start | bytes 884744 | tf_op jit(solution)/shard_map/ppermute | solution.py:121
  119.2 36.6 %collective-permute-start.9 = (f32[3,16,1536]{2,1,0:T(8,128)S(1)}, f32[3,16,1536]{2,1,0:T(8,128)S(1)}, u32[]{:S(2)}, u32[]{:S(2)}) collective-permute-start(f32[3,16,1536]{2,1,0:T(8,128)S(1)} %maximum_select_fusion), channel_id=1, source_target_pairs={{0,1},{1,0},{2,3},{3,2},{4,5},{5,4},{6,7},{7,6},{8,9},{9,8},{10,11... | collective-permute-start | bytes 884744 | tf_op jit(solution)/shard_map/ppermute | solution.py:121
  120.6 33.9 %collective-permute-start.11 = (f32[3,16,1536]{2,1,0:T(8,128)S(1)}, f32[3,16,1536]{2,1,0:T(8,128)S(1)}, u32[]{:S(2)}, u32[]{:S(2)}) collective-permute-start(f32[3,16,1536]{2,1,0:T(8,128)S(1)} %maximum_select_fusion.1), channel_id=1, source_target_pairs={{0,2},{1,3},{2,0},{3,1},{4,6},{5,7},{6,4},{7,5},{8,10},{9,11},{10,... | collective-permute-start | bytes 884744 | tf_op jit(solution)/shard_map/ppermute | solution.py:121
  135.9 17.2 %collective-permute-start.13 = (f32[3,16,1536]{2,1,0:T(8,128)S(1)}, f32[3,16,1536]{2,1,0:T(8,128)S(1)}, u32[]{:S(2)}, u32[]{:S(2)}) collective-permute-start(f32[3,16,1536]{2,1,0:T(8,128)S(1)} %maximum_select_fusion.2), channel_id=1, source_target_pairs={{0,3},{1,2},{2,1},{3,0},{4,7},{5,6},{6,5},{7,4},{8,11},{9,10},{10,... | collective-permute-start | bytes 884744 | tf_op jit(solution)/shard_map/ppermute | solution.py:121
  140.8 11.0 %collective-permute-start.15 = (f32[3,16,1536]{2,1,0:T(8,128)S(1)}, f32[3,16,1536]{2,1,0:T(8,128)S(1)}, u32[]{:S(2)}, u32[]{:S(2)}) collective-permute-start(f32[3,16,1536]{2,1,0:T(8,128)S(1)} %maximum_select_fusion.3), channel_id=1, source_target_pairs={{0,7},{1,6},{2,5},{3,4},{4,3},{5,2},{6,1},{7,0},{8,15},{9,14},{10,... | collective-permute-start | bytes 884744 | tf_op jit(solution)/shard_map/ppermute | solution.py:121
  145.4 1.0 copy-start

commit v2 on v1

v2 whole, which is shorter than its diff:
```python
import functools

import jax
import jax.numpy as jnp
from jax import lax
from jax.experimental import pallas as pl
from jax.experimental.pallas import tpu as pltpu
from jax.sharding import PartitionSpec as P


first_correction = 1.0 - 0.9**10
second_correction = 1.0 - 0.999**10

MIB = 1024 * 1024
LOAD_MIB, MERGE_MIB, ADAM_MIB = 12, 2, 8


def partner(index, step, size):
    if size & (size - 1) == 0:
        return index ^ step
    return (step - index) % size


def load_kernel(chips, count, pick_ref, *refs):
    own, near, outs = refs[:3], refs[3:6], refs[6:]
    for d in range(chips):
        for k in range(count):
            at = pick_ref[d * count + k]
            out = outs[d * count + k]

            @pl.when(at < count)
            def _():
                for j in range(3):
                    out[j] = own[j][at]

            @pl.when(at >= count)
            def _():
                for j in range(3):
                    out[j] = near[j][at - count]


def merge_kernel(chips, lag_ref, *refs):
    out_ref = refs[-1]
    for d in range(chips):

        @pl.when(lag_ref[0] == d)
        def _():
            out_ref[...] = refs[d][...]


def adam_kernel(groups, rows, place_ref, count_ref, grad_ref, *refs):
    pieces = refs[:groups]
    master_out, first_out, second_out = refs[groups:]
    slot_count = count_ref[0]
    for k in range(groups):
        here = pl.ds(pl.multiple_of(place_ref[k] * rows, rows), rows)
        master = pieces[k][0]
        first = pieces[k][1]
        second = pieces[k][2]
        scaled = grad_ref[0, here, :].astype(jnp.float32) / slot_count
        new_first = 0.9 * first + 0.1 * scaled
        new_second = 0.999 * second + 0.001 * scaled * scaled
        step_dir = new_first / first_correction / (jnp.sqrt(new_second / second_correction) + 1e-08)
        master_out[0, here, :] = master - 0.01 * (step_dir + 0.1 * master)
        first_out[0, here, :] = new_first
        second_out[0, here, :] = new_second


def body(order_k, old_master, old_first, old_second, new_grad, counts, old_owner, new_owner):
    groups_x = lax.axis_size("gx")
    groups_y = lax.axis_size("gy")
    held, rows, width = old_master.shape
    cores = 2 if groups_x % 2 == 0 else 1
    chips = groups_x // cores
    x = lax.axis_index("gx")
    y = lax.axis_index("gy")
    chip, core = x // cores, x % cores
    swap = [(i, (i // cores) * cores + (cores - 1 - i % cores)) for i in range(groups_x)]
    across = [
        [(i, ((i // cores + d) % chips) * cores + i % cores) for i in range(groups_x)]
        for d in range(1, chips)
    ]
    vm = pl.BlockSpec(memory_space=pltpu.VMEM)
    sm = pl.BlockSpec(memory_space=pltpu.SMEM)

    own = (old_master, old_first, old_second)
    if cores == 2:
        near = tuple(lax.ppermute(state, "gx", swap) for state in own)
    else:
        near = own

    step_k = jnp.array(order_k, dtype=jnp.int32)
    order = partner(y, step_k, groups_y)
    shift = jnp.arange(chips, dtype=jnp.int32)
    columns = ((chip + shift) % chips) * cores + core
    slots = columns[:, None] * groups_y + order[None, :]
    onehot = new_owner[:, None, None] == slots[None]
    source = jnp.sum(jnp.where(onehot, old_owner[:, None, None], 0), axis=0)
    from_x = source // held
    pick = source % held + jnp.where(from_x % cores == core, 0, held)
    lag = (chip - from_x[0] // cores + chips) % chips

    tally = counts[:, 0].astype(jnp.float32)
    for pairs in across:
        tally = tally + lax.ppermute(counts[:, 0].astype(jnp.float32), "gx", pairs)
    if cores == 2:
        tally = tally + lax.ppermute(tally, "gx", swap)

    piece = jax.ShapeDtypeStruct((3, rows, width), jnp.float32)
    loaded = list(pl.pallas_call(
        functools.partial(load_kernel, chips, held),
        out_shape=[piece] * (chips * held),
        in_specs=[sm] + [vm] * 6,
        out_specs=[vm] * (chips * held),
        compiler_params=pltpu.CompilerParams(vmem_limit_bytes=LOAD_MIB * MIB),
    )(pick.reshape(-1), *own, *near))

    tally, loaded[0] = lax.optimization_barrier((tally, loaded[0]))
    if groups_y & (groups_y - 1) == 0:
        step = 1
        while step < groups_y:
            tally = tally + lax.ppermute(tally, "gy", [(i, i ^ step) for i in range(groups_y)])
            step *= 2
    else:
        tally = lax.psum(tally, "gy")
    my_slot = x * groups_y + y
    slot_count = jnp.sum(jnp.where(new_owner == my_slot, tally, jnp.float32(0.0))).reshape(1)

    arrived = []
    for n, k in enumerate(order_k):
        sent = []
        for d in range(1, chips):
            sent.append(lax.ppermute(loaded[d * held + n], "gx", across[d - 1]))
        merged = pl.pallas_call(
            functools.partial(merge_kernel, chips),
            out_shape=piece,
            in_specs=[sm] + [vm] * chips,
            out_specs=vm,
            compiler_params=pltpu.CompilerParams(vmem_limit_bytes=MERGE_MIB * MIB),
        )(lax.dynamic_slice_in_dim(lag, n, 1), loaded[n], *sent)
        pairs = [(i, partner(i, k, groups_y)) for i in range(groups_y)]
        if any(a != b for a, b in pairs):
            merged = lax.ppermute(merged, "gy", pairs)
        arrived.append(merged)

    out = jax.ShapeDtypeStruct(new_grad.shape, jnp.float32)
    return tuple(
        pl.pallas_call(
            functools.partial(adam_kernel, groups_y, rows),
            out_shape=[out] * 3,
            in_specs=[sm, sm, vm] + [vm] * groups_y,
            out_specs=[vm] * 3,
            compiler_params=pltpu.CompilerParams(vmem_limit_bytes=ADAM_MIB * MIB),
        )(order, slot_count, new_grad, *arrived)
    )


def solution(mesh):
    groups_y = mesh.shape["gy"]
    half = groups_y // 2
    order_k = list(range(1, half)) + list(range(groups_y - 1, half - 1, -1)) + [0]

    def stepped(*args):
        return body(order_k, *args)

    placed = (
        P("gx", "gy", None),
        P("gx", "gy", None),
        P("gx", "gy", None),
        P(("gx", "gy"), None, None),
        P(None, ("gx", "gy")),
        P(),
        P(),
    )
    return jax.shard_map(
        stepped,
        mesh=mesh,
        in_specs=placed,
        out_specs=(
            P(("gx", "gy"), None, None),
            P(("gx", "gy"), None, None),
            P(("gx", "gy"), None, None),
        ),
        check_vma=False,
    )
```

time: 158 us -> 106 us (0.67)
  between operations: 35.9 us -> 0.76 us
  other arithmetic: 33.9 us -> 1.68 us
  waiting for transfers between devices: 37.9 us -> 50.3 us
  local copies, waits for them, and re-layouts: 3.85 us -> 5.97 us
    select_n x15 -> x2, other arithmetic: 32.1 us -> 0.03 us  [the longest x1 0.02 us: body(): lag = (chip - from_x[0] // cores + chips) % chips]
    ppermute x3, waiting for transfers between devices: 2.09 us -> 12.1 us  [body(): lax.ppermute(tally, 'gy', [(i, i ^ step) for i in range(groups_y)])]
    unnamed x14 -> x16, local copies, waits for them, and re-layouts: 1.65 us -> 5.21 us
    slice x3 -> x0, local copies, waits for them, and re-layouts: 2.12 us -> none  [the longest x1 0.73 us: held_piece(): is_own[d, k]]
    pallas_call x8 -> x10, Pallas kernels: 10.8 us -> 11.4 us  [the longest x8 6.94 us: body(): pl.pallas_call(functools.partial(merge_kernel, chips), out_shape=piece, i...]
  transfers between devices with their start and end apart: 23 -> 23, of which waited for: 10 -> 13; matrix products, arithmetic and copies ran while one was open for 19% -> 2% of each run, Pallas kernels for 6% -> 7%
where the time goes in v2:
time: 106 us
  waiting for transfers between devices  50.3 us (47%)
  starting transfers between devices  35.6 us (34%)
  Pallas kernels  11.4 us (11%)
  local copies, waits for them, and re-layouts  5.97 us (6%)
  other arithmetic  1.68 us (2%)
    ppermute x8, waiting for transfers between devices, body(): sent.append(lax.ppermute(loaded[d * held + n], 'gx', across[d - 1]))  19.6 us
    ppermute x7, waiting for transfers between devices, body(): merged = lax.ppermute(merged, 'gy', pairs)  17.6 us
    ppermute x7, starting transfers between devices, body(): merged = lax.ppermute(merged, 'gy', pairs)  16.6 us
    ppermute x3, waiting for transfers between devices, body(): lax.ppermute(tally, 'gy', [(i, i ^ step) for i in range(groups_y)])  12.1 us
    ppermute x8, starting transfers between devices, body(): sent.append(lax.ppermute(loaded[d * held + n], 'gx', across[d - 1]))  9.58 us
    pallas_call x8, Pallas kernels, body(): pl.pallas_call(functools.partial(merge_kernel, chips), out_shape=piece, i...  6.94 us
    ppermute x3, starting transfers between devices, body(): lax.ppermute(tally, 'gy', [(i, i ^ step) for i in range(groups_y)])  5.66 us
    unnamed x16, local copies, waits for them, and re-layouts  5.21 us
  transfers between devices with their start and end apart: 23, of which 13 were waited for; matrix products, arithmetic and copies ran while one was open for 2% of the time, Pallas kernels for 7%

profile of v2, /device:TPU:0, one launch (start us, length us, event | category | flops | bytes accessed | tf_op | source)
XLA Modules:
  0.0 105.8 jit_solution(3009403843423983752)
XLA Ops:
  0.6 0.6 collective-permute-start.2
  1.2 0.1 collective-permute-start.3
  1.3 0.4 collective-permute-start.4
  1.7 0.7 convert_bitcast_fusion
  2.4 2.6 %collective-permute-start = (f32[32]{0:T(128)S(1)}, f32[32]{0:T(128)S(1)}, u32[]{:S(2)}, u32[]{:S(2)}) collective-permute-start(f32[32]{0:T(128)S(1)} %convert_bitcast_fusion), channel_id=1, source_target_pairs={{0,16},{8,24},{16,0},{24,8},{1,17},{9,25},{17,1},{25,9},{2,18},{10... | collective-permute-start | bytes 392 | tf_op jit(solution)/shard_map/ppermute | solution.py:105
  5.0 0.6 copy-done.7
  5.6 0.1 broadcast_add_fusion
  5.7 0.6 copy-done.4
  6.3 0.0 copy-done.5
  6.3 0.2 select_reduce_fusion
  6.5 0.0 copy-start.6
  6.5 0.1 reduce_sum.21
  6.6 0.6 copy-done.6
  7.2 0.1 collective-permute-start.1
  7.3 1.0 collective-permute-done.1
  8.3 0.0 collective-permute-done.4.refs_5_
  8.3 0.0 copy-start
  8.4 1.1 %copy-done = f32[8,16,1536]{2,1,0:T(8,128)S(1)} copy-done((f32[8,16,1536]{2,1,0:T(8,128)S(1)}, f32[8,16,1536]{2,1,0:T(8,128)}, u32[]{:S(2)}) %copy-start) | copy-done | bytes 786456
  9.5 1.1 %copy-done.1 = f32[8,16,1536]{2,1,0:T(8,128)S(1)} copy-done((f32[8,16,1536]{2,1,0:T(8,128)S(1)}, f32[8,16,1536]{2,1,0:T(8,128)}, u32[]{:S(2)}) %copy-start.1) | copy-done | bytes 786456
  10.6 1.1 %copy-done.2 = f32[8,16,1536]{2,1,0:T(8,128)S(1)} copy-done((f32[8,16,1536]{2,1,0:T(8,128)S(1)}, f32[8,16,1536]{2,1,0:T(8,128)}, u32[]{:S(2)}) %copy-start.2) | copy-done | bytes 786456
  11.7 1.1 %shard_map.103 = (f32[3,16,1536]{2,1,0:T(8,128)S(1)}, f32[3,16,1536]{2,1,0:T(8,128)S(1)}, f32[3,16,1536]{2,1,0:T(8,128)S(1)}, f32[3,16,1536]{2,1,0:T(8,128)S(1)}...) custom-call(s32[16]{0:T(128)S(1)} %fusion.pick_ref, ...), custom_call_target="tpu_custom_call" | custom-call | tf_op jit(solution)/shard_map/pallas_call | solution.py:110
  12.8 1.4 %collective-permute-start.20 = (f32[3,16,1536]{2,1,0:T(8,128)S(1)}, f32[3,16,1536]{2,1,0:T(8,128)S(1)}, u32[]{:S(2)}, u32[]{:S(2)}) collective-permute-start(f32[3,16,1536]{2,1,0:T(8,128)S(1)} %get-tuple-element.36), channel_id=1, source_target_pairs={{0,16},{8,24},{16,0},{24,8},{1,17},{9,25},{17,1},{25,9},{2,18},{10... | collective-permute-start | bytes 884744 | tf_op jit(solution)/shard_map/ppermute | solution.py:133
  14.2 0.7 collective-permute-start.18
  14.9 1.5 %collective-permute-start.5 = (f32[32]{0:T(128)S(1)}, f32[32]{0:T(128)S(1)}, u32[]{:S(2)}, u32[]{:S(2)}) collective-permute-start(f32[32]{0:T(128)S(1)} %add.100), channel_id=1, source_target_pairs={{0,1},{1,0},{2,3},{3,2},{4,5},{5,4},{6,7},{7,6},{8,9},{9,8},{10,11... | collective-permute-start | bytes 392 | tf_op jit(solution)/shard_map/ppermute | solution.py:122
  16.4 1.4 %collective-permute-start.16 = (f32[3,16,1536]{2,1,0:T(8,128)S(1)}, f32[3,16,1536]{2,1,0:T(8,128)S(1)}, u32[]{:S(2)}, u32[]{:S(2)}) collective-permute-start(f32[3,16,1536]{2,1,0:T(8,128)S(1)} %get-tuple-element.32), channel_id=1, source_target_pairs={{0,16},{8,24},{16,0},{24,8},{1,17},{9,25},{17,1},{25,9},{2,18},{10... | collective-permute-start | bytes 884744 | tf_op jit(solution)/shard_map/ppermute | solution.py:133
  17.8 0.7 collective-permute-done.5
  18.5 1.6 %collective-permute-start.6 = (f32[32]{0:T(128)S(1)}, f32[32]{0:T(128)S(1)}, u32[]{:S(2)}, u32[]{:S(2)}) collective-permute-start(f32[32]{0:T(128)S(1)} %add.113), channel_id=1, source_target_pairs={{0,2},{1,3},{2,0},{3,1},{4,6},{5,7},{6,4},{7,5},{8,10},{9,11},{10,... | collective-permute-start | bytes 392 | tf_op jit(solution)/shard_map/ppermute | solution.py:122
  20.1 1.4 %collective-permute-start.14 = (f32[3,16,1536]{2,1,0:T(8,128)S(1)}, f32[3,16,1536]{2,1,0:T(8,128)S(1)}, u32[]{:S(2)}, u32[]{:S(2)}) collective-permute-start(f32[3,16,1536]{2,1,0:T(8,128)S(1)} %get-tuple-element.30), channel_id=1, source_target_pairs={{0,16},{8,24},{16,0},{24,8},{1,17},{9,25},{17,1},{25,9},{2,18},{10... | collective-permute-start | bytes 884744 | tf_op jit(solution)/shard_map/ppermute | solution.py:133
  21.4 0.6 collective-permute-done.6
  22.1 1.4 %collective-permute-start.12 = (f32[3,16,1536]{2,1,0:T(8,128)S(1)}, f32[3,16,1536]{2,1,0:T(8,128)S(1)}, u32[]{:S(2)}, u32[]{:S(2)}) collective-permute-start(f32[3,16,1536]{2,1,0:T(8,128)S(1)} %get-tuple-element.28), channel_id=1, source_target_pairs={{0,16},{8,24},{16,0},{24,8},{1,17},{9,25},{17,1},{25,9},{2,18},{10... | collective-permute-start | bytes 884744 | tf_op jit(solution)/shard_map/ppermute | solution.py:133
  23.4 0.7 fusion.9
  24.1 0.0 collective-permute-done.20.refs_1_
  24.1 0.7 collective-permute-start.10
  24.8 4.3 %collective-permute-done.18.refs_1_ = f32[3,16,1536]{2,1,0:T(8,128)S(1)} collective-permute-done((f32[3,16,1536]{2,1,0:T(8,128)S(1)}, f32[3,16,1536]{2,1,0:T(8,128)S(1)}, u32[]{:S(2)}, u32[]{:S(2)}) %collective-permute-start.18) | collective-permute-done | bytes 294944 | tf_op jit(solution)/shard_map/ppermute | solution.py:133
  29.1 1.4 %collective-permute-start.8 = (f32[3,16,1536]{2,1,0:T(8,128)S(1)}, f32[3,16,1536]{2,1,0:T(8,128)S(1)}, u32[]{:S(2)}, u32[]{:S(2)}) collective-permute-start(f32[3,16,1536]{2,1,0:T(8,128)S(1)} %get-tuple-element.24), channel_id=1, source_target_pairs={{0,16},{8,24},{16,0},{24,8},{1,17},{9,25},{17,1},{25,9},{2,18},{10... | collective-permute-start | bytes 884744 | tf_op jit(solution)/shard_map/ppermute | solution.py:133
  30.4 0.7 shard_map.110
  31.1 0.7 shard_map.109
  31.8 3.6 %collective-permute-done.16.refs_1_ = f32[3,16,1536]{2,1,0:T(8,128)S(1)} collective-permute-done((f32[3,16,1536]{2,1,0:T(8,128)S(1)}, f32[3,16,1536]{2,1,0:T(8,128)S(1)}, u32[]{:S(2)}, u32[]{:S(2)}) %collective-permute-start.16) | collective-permute-done | bytes 294944 | tf_op jit(solution)/shard_map/ppermute | solution.py:133
  35.4 1.4 %collective-permute-start.22 = (f32[3,16,1536]{2,1,0:T(8,128)S(1)}, f32[3,16,1536]{2,1,0:T(8,128)S(1)}, u32[]{:S(2)}, u32[]{:S(2)}) collective-permute-start(f32[3,16,1536]{2,1,0:T(8,128)S(1)} %get-tuple-element.38), channel_id=1, source_target_pairs={{0,16},{8,24},{16,0},{24,8},{1,17},{9,25},{17,1},{25,9},{2,18},{10... | collective-permute-start | bytes 884744 | tf_op jit(solution)/shard_map/ppermute | solution.py:133
  36.8 5.0 %collective-permute-done.14.refs_1_ = f32[3,16,1536]{2,1,0:T(8,128)S(1)} collective-permute-done((f32[3,16,1536]{2,1,0:T(8,128)S(1)}, f32[3,16,1536]{2,1,0:T(8,128)S(1)}, u32[]{:S(2)}, u32[]{:S(2)}) %collective-permute-start.14) | collective-permute-done | bytes 294944 | tf_op jit(solution)/shard_map/ppermute | solution.py:133
  41.7 2.6 %collective-permute-start.21 = (f32[3,16,1536]{2,1,0:T(8,128)S(1)}, f32[3,16,1536]{2,1,0:T(8,128)S(1)}, u32[]{:S(2)}, u32[]{:S(2)}) collective-permute-start(f32[3,16,1536]{2,1,0:T(8,128)S(1)} %shard_map.110), channel_id=1, source_target_pairs={{0,4},{1,5},{2,6},{3,7},{4,0},{5,1},{6,2},{7,3},{8,12},{9,13},{10,... | collective-permute-start | bytes 884744 | tf_op jit(solution)/shard_map/ppermute | solution.py:143
  44.3 3.7 %collective-permute-done.12.refs_1_ = f32[3,16,1536]{2,1,0:T(8,128)S(1)} collective-permute-done((f32[3,16,1536]{2,1,0:T(8,128)S(1)}, f32[3,16,1536]{2,1,0:T(8,128)S(1)}, u32[]{:S(2)}, u32[]{:S(2)}) %collective-permute-start.12) | collective-permute-done | bytes 294944 | tf_op jit(solution)/shard_map/ppermute | solution.py:133
  48.0 3.5 %collective-permute-start.19 = (f32[3,16,1536]{2,1,0:T(8,128)S(1)}, f32[3,16,1536]{2,1,0:T(8,128)S(1)}, u32[]{:S(2)}, u32[]{:S(2)}) collective-permute-start(f32[3,16,1536]{2,1,0:T(8,128)S(1)} %shard_map.109), channel_id=1, source_target_pairs={{0,5},{1,4},{2,7},{3,6},{4,1},{5,0},{6,3},{7,2},{8,13},{9,12},{10,... | collective-permute-start | bytes 884744 | tf_op jit(solution)/shard_map/ppermute | solution.py:143
  51.6 0.7 shard_map.108
  52.3 0.7 shard_map.107
  53.0 0.7 shard_map.106
  53.7 0.7 collective-permute-done.10.refs_1_
  54.4 2.6 %collective-permute-start.7 = (f32[32]{0:T(128)S(1)}, f32[32]{0:T(128)S(1)}, u32[]{:S(2)}, u32[]{:S(2)}) collective-permute-start(f32[32]{0:T(128)S(1)} %add.114), channel_id=1, source_target_pairs={{0,4},{1,5},{2,6},{3,7},{4,0},{5,1},{6,2},{7,3},{8,12},{9,13},{10,... | collective-permute-start | bytes 392 | tf_op jit(solution)/shard_map/ppermute | solution.py:122
  57.0 1.4 %shard_map.105 = f32[3,16,1536]{2,1,0:T(8,128)} custom-call(s32[1]{0:T(128)} %get-tuple-element.45.lag_ref, f32[3,16,1536]{2,1,0:T(8,128)S(1)} %get-tuple-element.25.refs_0_, f32[3,16,1536]{2,1,0:T(8,128)S(1)} %collective-permute-done.10.refs_1_), custom_call_target="tpu_custom_call" | custom-call | tf_op jit(solution)/shard_map/pallas_call | solution.py:134
  58.3 2.4 %collective-permute-done.8.refs_1_ = f32[3,16,1536]{2,1,0:T(8,128)S(1)} collective-permute-done((f32[3,16,1536]{2,1,0:T(8,128)S(1)}, f32[3,16,1536]{2,1,0:T(8,128)S(1)}, u32[]{:S(2)}, u32[]{:S(2)}) %collective-permute-start.8) | collective-permute-done | bytes 294944 | tf_op jit(solution)/shard_map/ppermute | solution.py:133
  60.7 3.6 %collective-permute-start.17 = (f32[3,16,1536]{2,1,0:T(8,128)S(1)}, f32[3,16,1536]{2,1,0:T(8,128)S(1)}, u32[]{:S(2)}, u32[]{:S(2)}) collective-permute-start(f32[3,16,1536]{2,1,0:T(8,128)S(1)} %shard_map.108), channel_id=1, source_target_pairs={{0,6},{1,7},{2,4},{3,5},{4,2},{5,3},{6,0},{7,1},{8,14},{9,15},{10,... | collective-permute-start | bytes 884744 | tf_op jit(solution)/shard_map/ppermute | solution.py:143
  64.3 1.4 %shard_map.104 = f32[3,16,1536]{2,1,0:T(8,128)} custom-call(s32[1]{0:T(128)} %get-tuple-element.46.lag_ref, f32[3,16,1536]{2,1,0:T(8,128)S(1)} %get-tuple-element.23.refs_0_, f32[3,16,1536]{2,1,0:T(8,128)S(1)} %collective-permute-done.8.refs_1_), custom_call_target="tpu_custom_call" | custom-call | tf_op jit(solution)/shard_map/pallas_call | solution.py:134
  65.7 10.7 %collective-permute-done.7 = f32[32]{0:T(128)S(1)} collective-permute-done((f32[32]{0:T(128)S(1)}, f32[32]{0:T(128)S(1)}, u32[]{:S(2)}, u32[]{:S(2)}) %collective-permute-start.7) | collective-permute-done | bytes 160 | tf_op jit(solution)/shard_map/ppermute | solution.py:122
  76.5 3.4 %collective-permute-start.15 = (f32[3,16,1536]{2,1,0:T(8,128)S(1)}, f32[3,16,1536]{2,1,0:T(8,128)S(1)}, u32[]{:S(2)}, u32[]{:S(2)}) collective-permute-start(f32[3,16,1536]{2,1,0:T(8,128)S(1)} %shard_map.107), channel_id=1, source_target_pairs={{0,7},{1,6},{2,5},{3,4},{4,3},{5,2},{6,1},{7,0},{8,15},{9,14},{10,... | collective-permute-start | bytes 884744 | tf_op jit(solution)/shard_map/ppermute | solution.py:143
  79.9 0.0 collective-permute-start.13
  79.9 0.0 collective-permute-done.21.refs_6_
  79.9 2.0 %collective-permute-start.11 = (f32[3,16,1536]{2,1,0:T(8,128)}, f32[3,16,1536]{2,1,0:T(8,128)S(1)}, u32[]{:S(2)}, u32[]{:S(2)}) collective-permute-start(f32[3,16,1536]{2,1,0:T(8,128)} %shard_map.105), channel_id=1, source_target_pairs={{0,2},{1,3},{2,0},{3,1},{4,6},{5,7},{6,4},{7,5},{8,10},{9,11},{10,... | collective-permute-start | bytes 884744 | tf_op jit(solution)/shard_map/ppermute | solution.py:143
  81.9 1.5 %collective-permute-start.9 = (f32[3,16,1536]{2,1,0:T(8,128)}, f32[3,16,1536]{2,1,0:T(8,128)S(1)}, u32[]{:S(2)}, u32[]{:S(2)}) collective-permute-start(f32[3,16,1536]{2,1,0:T(8,128)} %shard_map.104), channel_id=1, source_target_pairs={{0,1},{1,0},{2,3},{3,2},{4,5},{5,4},{6,7},{7,6},{8,9},{9,8},{10,11... | collective-permute-start | bytes 884744 | tf_op jit(solution)/shard_map/ppermute | solution.py:143
  83.4 0.7 fusion.1
  84.0 0.7 shard_map.111.refs_7_
  84.8 4.3 %collective-permute-done.15.refs_3_ = f32[3,16,1536]{2,1,0:T(8,128)S(1)} collective-permute-done((f32[3,16,1536]{2,1,0:T(8,128)S(1)}, f32[3,16,1536]{2,1,0:T(8,128)S(1)}, u32[]{:S(2)}, u32[]{:S(2)}) %collective-permute-start.15) | collective-permute-done | bytes 294944 | tf_op jit(solution)/shard_map/ppermute | solution.py:143
  89.1 7.8 %collective-permute-done.13.refs_2_ = f32[3,16,1536]{2,1,0:T(8,128)S(1)} collective-permute-done((f32[3,16,1536]{2,1,0:T(8,128)S(1)}, f32[3,16,1536]{2,1,0:T(8,128)S(1)}, u32[]{:S(2)}, u32[]{:S(2)}) %collective-permute-start.13) | collective-permute-done | bytes 294944 | tf_op jit(solution)/shard_map/ppermute | solution.py:143
  96.9 5.4 %collective-permute-done.11.refs_1_ = f32[3,16,1536]{2,1,0:T(8,128)S(1)} collective-permute-done((f32[3,16,1536]{2,1,0:T(8,128)}, f32[3,16,1536]{2,1,0:T(8,128)S(1)}, u32[]{:S(2)}, u32[]{:S(2)}) %collective-permute-start.11) | collective-permute-done | bytes 294944 | tf_op jit(solution)/shard_map/ppermute | solution.py:143
  102.4 3.4 %shard_map.112 = (f32[1,128,1536]{2,1,0:T(8,128)}, f32[1,128,1536]{2,1,0:T(8,128)}, f32[1,128,1536]{2,1,0:T(8,128)}) custom-call(s32[8]{0:T(128)S(1)} %broadcast_xor_fusion.place_ref, f32[1]{0:T(128)} %bitcast.1.count_ref, bf16[1,128,1536]{2,1,0:T(8,128)(2,1)S(1)} %copy-done.3, f32[3,16,1536]{2,1,0:T(8,128)S(1)} %collective-permute-done.9.refs_0_, ...), custom_call_target="tpu_custom_call" | custom-call | tf_op jit(solution)/shard_map/pallas_call | solution.py:148
  (23 shorter events, 0.1 us)
Async XLA Ops:
  0.6 7.7 %collective-permute-start.2 = (f32[8,16,1536]{2,1,0:T(8,128)}, f32[8,16,1536]{2,1,0:T(8,128)S(1)}, u32[]{:S(2)}, u32[]{:S(2)}) collective-permute-start(f32[8,16,1536]{2,1,0:T(8,128)} %refs_0_.1), channel_id=1, source_target_pairs={{0,8},{8,0},{16,24},{24,16},{1,9},{9,1},{17,25},{25,17},{2,10},{10... | collective-permute-start | bytes 2359304 | tf_op jit(solution)/shard_map/ppermute | solution.py:88
  1.2 7.1 %collective-permute-start.3 = (f32[8,16,1536]{2,1,0:T(8,128)}, f32[8,16,1536]{2,1,0:T(8,128)S(1)}, u32[]{:S(2)}, u32[]{:S(2)}) collective-permute-start(f32[8,16,1536]{2,1,0:T(8,128)} %refs_1_.1), channel_id=1, source_target_pairs={{0,8},{8,0},{16,24},{24,16},{1,9},{9,1},{17,25},{25,17},{2,10},{10... | collective-permute-start | bytes 2359304 | tf_op jit(solution)/shard_map/ppermute | solution.py:88
  1.3 7.1 %collective-permute-start.4 = (f32[8,16,1536]{2,1,0:T(8,128)}, f32[8,16,1536]{2,1,0:T(8,128)S(1)}, u32[]{:S(2)}, u32[]{:S(2)}) collective-permute-start(f32[8,16,1536]{2,1,0:T(8,128)} %refs_2_.1), channel_id=1, source_target_pairs={{0,8},{8,0},{16,24},{24,16},{1,9},{9,1},{17,25},{25,17},{2,10},{10... | collective-permute-start | bytes 2359304 | tf_op jit(solution)/shard_map/ppermute | solution.py:88
  2.4 4.2 %collective-permute-start = (f32[32]{0:T(128)S(1)}, f32[32]{0:T(128)S(1)}, u32[]{:S(2)}, u32[]{:S(2)}) collective-permute-start(f32[32]{0:T(128)S(1)} %convert_bitcast_fusion), channel_id=1, source_target_pairs={{0,16},{8,24},{16,0},{24,8},{1,17},{9,25},{17,1},{25,9},{2,18},{10... | collective-permute-start | bytes 392 | tf_op jit(solution)/shard_map/ppermute | solution.py:105
  4.9 0.7 copy-start.7
  5.6 0.7 copy-start.4
  5.6 0.7 copy-start.5
  6.5 0.7 copy-start.6
  7.2 1.2 %collective-permute-start.1 = (f32[32]{0:T(128)S(1)}, f32[32]{0:T(128)S(1)}, u32[]{:S(2)}, u32[]{:S(2)}) collective-permute-start(f32[32]{0:T(128)S(1)} %fusion.8), channel_id=1, source_target_pairs={{0,8},{8,0},{16,24},{24,16},{1,9},{9,1},{17,25},{25,17},{2,10},{10... | collective-permute-start | bytes 392 | tf_op jit(solution)/shard_map/ppermute | solution.py:107
  8.3 1.1 %copy-start = (f32[8,16,1536]{2,1,0:T(8,128)S(1)}, f32[8,16,1536]{2,1,0:T(8,128)}, u32[]{:S(2)}) copy-start(f32[8,16,1536]{2,1,0:T(8,128)} %refs_0_.1) | copy-start | bytes 2359300
  9.5 1.1 %copy-start.1 = (f32[8,16,1536]{2,1,0:T(8,128)S(1)}, f32[8,16,1536]{2,1,0:T(8,128)}, u32[]{:S(2)}) copy-start(f32[8,16,1536]{2,1,0:T(8,128)} %refs_1_.1) | copy-start | bytes 2359300
  10.6 1.1 %copy-start.2 = (f32[8,16,1536]{2,1,0:T(8,128)S(1)}, f32[8,16,1536]{2,1,0:T(8,128)}, u32[]{:S(2)}) copy-start(f32[8,16,1536]{2,1,0:T(8,128)} %refs_2_.1) | copy-start | bytes 2359300
  12.8 11.3 %collective-permute-start.20 = (f32[3,16,1536]{2,1,0:T(8,128)S(1)}, f32[3,16,1536]{2,1,0:T(8,128)S(1)}, u32[]{:S(2)}, u32[]{:S(2)}) collective-permute-start(f32[3,16,1536]{2,1,0:T(8,128)S(1)} %get-tuple-element.36), channel_id=1, source_target_pairs={{0,16},{8,24},{16,0},{24,8},{1,17},{9,25},{17,1},{25,9},{2,18},{10... | collective-permute-start | bytes 884744 | tf_op jit(solution)/shard_map/ppermute | solution.py:133
  14.2 14.8 %collective-permute-start.18 = (f32[3,16,1536]{2,1,0:T(8,128)S(1)}, f32[3,16,1536]{2,1,0:T(8,128)S(1)}, u32[]{:S(2)}, u32[]{:S(2)}) collective-permute-start(f32[3,16,1536]{2,1,0:T(8,128)S(1)} %get-tuple-element.34), channel_id=1, source_target_pairs={{0,16},{8,24},{16,0},{24,8},{1,17},{9,25},{17,1},{25,9},{2,18},{10... | collective-permute-start | bytes 884744 | tf_op jit(solution)/shard_map/ppermute | solution.py:133
  14.9 3.6 %collective-permute-start.5 = (f32[32]{0:T(128)S(1)}, f32[32]{0:T(128)S(1)}, u32[]{:S(2)}, u32[]{:S(2)}) collective-permute-start(f32[32]{0:T(128)S(1)} %add.100), channel_id=1, source_target_pairs={{0,1},{1,0},{2,3},{3,2},{4,5},{5,4},{6,7},{7,6},{8,9},{9,8},{10,11... | collective-permute-start | bytes 392 | tf_op jit(solution)/shard_map/ppermute | solution.py:122
  16.4 19.0 %collective-permute-start.16 = (f32[3,16,1536]{2,1,0:T(8,128)S(1)}, f32[3,16,1536]{2,1,0:T(8,128)S(1)}, u32[]{:S(2)}, u32[]{:S(2)}) collective-permute-start(f32[3,16,1536]{2,1,0:T(8,128)S(1)} %get-tuple-element.32), channel_id=1, source_target_pairs={{0,16},{8,24},{16,0},{24,8},{1,17},{9,25},{17,1},{25,9},{2,18},{10... | collective-permute-start | bytes 884744 | tf_op jit(solution)/shard_map/ppermute | solution.py:133
  18.5 3.6 %collective-permute-start.6 = (f32[32]{0:T(128)S(1)}, f32[32]{0:T(128)S(1)}, u32[]{:S(2)}, u32[]{:S(2)}) collective-permute-start(f32[32]{0:T(128)S(1)} %add.113), channel_id=1, source_target_pairs={{0,2},{1,3},{2,0},{3,1},{4,6},{5,7},{6,4},{7,5},{8,10},{9,11},{10,... | collective-permute-start | bytes 392 | tf_op jit(solution)/shard_map/ppermute | solution.py:122
  20.1 21.7 %collective-permute-start.14 = (f32[3,16,1536]{2,1,0:T(8,128)S(1)}, f32[3,16,1536]{2,1,0:T(8,128)S(1)}, u32[]{:S(2)}, u32[]{:S(2)}) collective-permute-start(f32[3,16,1536]{2,1,0:T(8,128)S(1)} %get-tuple-element.30), channel_id=1, source_target_pairs={{0,16},{8,24},{16,0},{24,8},{1,17},{9,25},{17,1},{25,9},{2,18},{10... | collective-permute-start | bytes 884744 | tf_op jit(solution)/shard_map/ppermute | solution.py:133
  22.1 26.0 %collective-permute-start.12 = (f32[3,16,1536]{2,1,0:T(8,128)S(1)}, f32[3,16,1536]{2,1,0:T(8,128)S(1)}, u32[]{:S(2)}, u32[]{:S(2)}) collective-permute-start(f32[3,16,1536]{2,1,0:T(8,128)S(1)} %get-tuple-element.28), channel_id=1, source_target_pairs={{0,16},{8,24},{16,0},{24,8},{1,17},{9,25},{17,1},{25,9},{2,18},{10... | collective-permute-start | bytes 884744 | tf_op jit(solution)/shard_map/ppermute | solution.py:133
  24.1 30.2 %collective-permute-start.10 = (f32[3,16,1536]{2,1,0:T(8,128)S(1)}, f32[3,16,1536]{2,1,0:T(8,128)S(1)}, u32[]{:S(2)}, u32[]{:S(2)}) collective-permute-start(f32[3,16,1536]{2,1,0:T(8,128)S(1)} %get-tuple-element.26), channel_id=1, source_target_pairs={{0,16},{8,24},{16,0},{24,8},{1,17},{9,25},{17,1},{25,9},{2,18},{10... | collective-permute-start | bytes 884744 | tf_op jit(solution)/shard_map/ppermute | solution.py:133
  29.1 31.6 %collective-permute-start.8 = (f32[3,16,1536]{2,1,0:T(8,128)S(1)}, f32[3,16,1536]{2,1,0:T(8,128)S(1)}, u32[]{:S(2)}, u32[]{:S(2)}) collective-permute-start(f32[3,16,1536]{2,1,0:T(8,128)S(1)} %get-tuple-element.24), channel_id=1, source_target_pairs={{0,16},{8,24},{16,0},{24,8},{1,17},{9,25},{17,1},{25,9},{2,18},{10... | collective-permute-start | bytes 884744 | tf_op jit(solution)/shard_map/ppermute | solution.py:133
  35.4 44.5 %collective-permute-start.22 = (f32[3,16,1536]{2,1,0:T(8,128)S(1)}, f32[3,16,1536]{2,1,0:T(8,128)S(1)}, u32[]{:S(2)}, u32[]{:S(2)}) collective-permute-start(f32[3,16,1536]{2,1,0:T(8,128)S(1)} %get-tuple-element.38), channel_id=1, source_target_pairs={{0,16},{8,24},{16,0},{24,8},{1,17},{9,25},{17,1},{25,9},{2,18},{10... | collective-permute-start | bytes 884744 | tf_op jit(solution)/shard_map/ppermute | solution.py:133
  41.7 38.1 %collective-permute-start.21 = (f32[3,16,1536]{2,1,0:T(8,128)S(1)}, f32[3,16,1536]{2,1,0:T(8,128)S(1)}, u32[]{:S(2)}, u32[]{:S(2)}) collective-permute-start(f32[3,16,1536]{2,1,0:T(8,128)S(1)} %shard_map.110), channel_id=1, source_target_pairs={{0,4},{1,5},{2,6},{3,7},{4,0},{5,1},{6,2},{7,3},{8,12},{9,13},{10,... | collective-permute-start | bytes 884744 | tf_op jit(solution)/shard_map/ppermute | solution.py:143
  48.0 33.8 %collective-permute-start.19 = (f32[3,16,1536]{2,1,0:T(8,128)S(1)}, f32[3,16,1536]{2,1,0:T(8,128)S(1)}, u32[]{:S(2)}, u32[]{:S(2)}) collective-permute-start(f32[3,16,1536]{2,1,0:T(8,128)S(1)} %shard_map.109), channel_id=1, source_target_pairs={{0,5},{1,4},{2,7},{3,6},{4,1},{5,0},{6,3},{7,2},{8,13},{9,12},{10,... | collective-permute-start | bytes 884744 | tf_op jit(solution)/shard_map/ppermute | solution.py:143
  54.4 22.1 %collective-permute-start.7 = (f32[32]{0:T(128)S(1)}, f32[32]{0:T(128)S(1)}, u32[]{:S(2)}, u32[]{:S(2)}) collective-permute-start(f32[32]{0:T(128)S(1)} %add.114), channel_id=1, source_target_pairs={{0,4},{1,5},{2,6},{3,7},{4,0},{5,1},{6,2},{7,3},{8,12},{9,13},{10,... | collective-permute-start | bytes 392 | tf_op jit(solution)/shard_map/ppermute | solution.py:122
  60.7 24.1 %collective-permute-start.17 = (f32[3,16,1536]{2,1,0:T(8,128)S(1)}, f32[3,16,1536]{2,1,0:T(8,128)S(1)}, u32[]{:S(2)}, u32[]{:S(2)}) collective-permute-start(f32[3,16,1536]{2,1,0:T(8,128)S(1)} %shard_map.108), channel_id=1, source_target_pairs={{0,6},{1,7},{2,4},{3,5},{4,2},{5,3},{6,0},{7,1},{8,14},{9,15},{10,... | collective-permute-start | bytes 884744 | tf_op jit(solution)/shard_map/ppermute | solution.py:143
  76.5 12.6 %collective-permute-start.15 = (f32[3,16,1536]{2,1,0:T(8,128)S(1)}, f32[3,16,1536]{2,1,0:T(8,128)S(1)}, u32[]{:S(2)}, u32[]{:S(2)}) collective-permute-start(f32[3,16,1536]{2,1,0:T(8,128)S(1)} %shard_map.107), channel_id=1, source_target_pairs={{0,7},{1,6},{2,5},{3,4},{4,3},{5,2},{6,1},{7,0},{8,15},{9,14},{10,... | collective-permute-start | bytes 884744 | tf_op jit(solution)/shard_map/ppermute | solution.py:143
  79.9 17.1 %collective-permute-start.13 = (f32[3,16,1536]{2,1,0:T(8,128)S(1)}, f32[3,16,1536]{2,1,0:T(8,128)S(1)}, u32[]{:S(2)}, u32[]{:S(2)}) collective-permute-start(f32[3,16,1536]{2,1,0:T(8,128)S(1)} %shard_map.106), channel_id=1, source_target_pairs={{0,3},{1,2},{2,1},{3,0},{4,7},{5,6},{6,5},{7,4},{8,11},{9,10},{10,... | collective-permute-start | bytes 884744 | tf_op jit(solution)/shard_map/ppermute | solution.py:143
  79.9 22.5 %collective-permute-start.11 = (f32[3,16,1536]{2,1,0:T(8,128)}, f32[3,16,1536]{2,1,0:T(8,128)S(1)}, u32[]{:S(2)}, u32[]{:S(2)}) collective-permute-start(f32[3,16,1536]{2,1,0:T(8,128)} %shard_map.105), channel_id=1, source_target_pairs={{0,2},{1,3},{2,0},{3,1},{4,6},{5,7},{6,4},{7,5},{8,10},{9,11},{10,... | collective-permute-start | bytes 884744 | tf_op jit(solution)/shard_map/ppermute | solution.py:143
  81.9 20.5 %collective-permute-start.9 = (f32[3,16,1536]{2,1,0:T(8,128)}, f32[3,16,1536]{2,1,0:T(8,128)S(1)}, u32[]{:S(2)}, u32[]{:S(2)}) collective-permute-start(f32[3,16,1536]{2,1,0:T(8,128)} %shard_map.104), channel_id=1, source_target_pairs={{0,1},{1,0},{2,3},{3,2},{4,5},{5,4},{6,7},{7,6},{8,9},{9,8},{10,11... | collective-permute-start | bytes 884744 | tf_op jit(solution)/shard_map/ppermute | solution.py:143
  84.0 18.3 %copy-start.3 = (bf16[1,128,1536]{2,1,0:T(8,128)(2,1)S(1)}, bf16[1,128,1536]{2,1,0:T(8,128)(2,1)}, u32[]{:S(2)}) copy-start(bf16[1,128,1536]{2,1,0:T(8,128)(2,1)} %grad_ref.1) | copy-start | bytes 1179652

commit v3 on v2

--- a/solution.py
+++ b/solution.py
@@ -117,10 +117,9 @@
 
     tally, loaded[0] = lax.optimization_barrier((tally, loaded[0]))
     if groups_y & (groups_y - 1) == 0:
-        step = 1
-        while step < groups_y:
-            tally = tally + lax.ppermute(tally, "gy", [(i, i ^ step) for i in range(groups_y)])
-            step *= 2
+        for hop in range(groups_y.bit_length() - 1):
+            pairs = [(i, i ^ (1 << hop)) for i in range(groups_y)]
+            tally = tally + lax.ppermute(tally, "gy", pairs)
     else:
         tally = lax.psum(tally, "gy")
     my_slot = x * groups_y + y

time: 106 us -> 106 us (level)
  no operation moved by 1% of the time
where the time goes in v3:
time: 106 us
  waiting for transfers between devices  50.3 us (47%)
  starting transfers between devices  35.6 us (34%)
  Pallas kernels  11.4 us (11%)
  local copies, waits for them, and re-layouts  5.97 us (6%)
  other arithmetic  1.68 us (2%)
    ppermute x8, waiting for transfers between devices, body(): sent.append(lax.ppermute(loaded[d * held + n], 'gx', across[d - 1]))  19.6 us
    ppermute x7, waiting for transfers between devices, body(): merged = lax.ppermute(merged, 'gy', pairs)  17.6 us
    ppermute x7, starting transfers between devices, body(): merged = lax.ppermute(merged, 'gy', pairs)  16.6 us
    ppermute x3, waiting for transfers between devices, body(): tally = tally + lax.ppermute(tally, 'gy', pairs)  12.1 us
    ppermute x8, starting transfers between devices, body(): sent.append(lax.ppermute(loaded[d * held + n], 'gx', across[d - 1]))  9.58 us
    pallas_call x8, Pallas kernels, body(): pl.pallas_call(functools.partial(merge_kernel, chips), out_shape=piece, i...  6.94 us
    ppermute x3, starting transfers between devices, body(): tally = tally + lax.ppermute(tally, 'gy', pairs)  5.66 us
    unnamed x16, local copies, waits for them, and re-layouts  5.21 us
  transfers between devices with their start and end apart: 23, of which 13 were waited for; matrix products, arithmetic and copies ran while one was open for 2% of the time, Pallas kernels for 7%

profile of v3, /device:TPU:0, one launch (start us, length us, event | category | flops | bytes accessed | tf_op | source)
XLA Modules:
  0.0 105.8 jit_solution(3009403843423983752)
XLA Ops:
  0.6 0.6 collective-permute-start.2
  1.2 0.1 collective-permute-start.3
  1.3 0.4 collective-permute-start.4
  1.7 0.7 convert_bitcast_fusion
  2.4 2.6 %collective-permute-start = (f32[32]{0:T(128)S(1)}, f32[32]{0:T(128)S(1)}, u32[]{:S(2)}, u32[]{:S(2)}) collective-permute-start(f32[32]{0:T(128)S(1)} %convert_bitcast_fusion), channel_id=1, source_target_pairs={{0,16},{8,24},{16,0},{24,8},{1,17},{9,25},{17,1},{25,9},{2,18},{10... | collective-permute-start | bytes 392 | tf_op jit(solution)/shard_map/ppermute | solution.py:105
  5.0 0.6 copy-done.7
  5.6 0.1 broadcast_add_fusion
  5.7 0.6 copy-done.4
  6.3 0.0 copy-done.5
  6.3 0.2 select_reduce_fusion
  6.5 0.0 copy-start.6
  6.5 0.1 reduce_sum.21
  6.6 0.6 copy-done.6
  7.2 0.1 collective-permute-start.1
  7.3 1.0 collective-permute-done.1
  8.3 0.0 collective-permute-done.4.refs_5_
  8.3 0.0 copy-start
  8.4 1.1 %copy-done = f32[8,16,1536]{2,1,0:T(8,128)S(1)} copy-done((f32[8,16,1536]{2,1,0:T(8,128)S(1)}, f32[8,16,1536]{2,1,0:T(8,128)}, u32[]{:S(2)}) %copy-start) | copy-done | bytes 786456
  9.5 1.1 %copy-done.1 = f32[8,16,1536]{2,1,0:T(8,128)S(1)} copy-done((f32[8,16,1536]{2,1,0:T(8,128)S(1)}, f32[8,16,1536]{2,1,0:T(8,128)}, u32[]{:S(2)}) %copy-start.1) | copy-done | bytes 786456
  10.6 1.1 %copy-done.2 = f32[8,16,1536]{2,1,0:T(8,128)S(1)} copy-done((f32[8,16,1536]{2,1,0:T(8,128)S(1)}, f32[8,16,1536]{2,1,0:T(8,128)}, u32[]{:S(2)}) %copy-start.2) | copy-done | bytes 786456
  11.7 1.1 %shard_map.103 = (f32[3,16,1536]{2,1,0:T(8,128)S(1)}, f32[3,16,1536]{2,1,0:T(8,128)S(1)}, f32[3,16,1536]{2,1,0:T(8,128)S(1)}, f32[3,16,1536]{2,1,0:T(8,128)S(1)}...) custom-call(s32[16]{0:T(128)S(1)} %fusion.pick_ref, ...), custom_call_target="tpu_custom_call" | custom-call | tf_op jit(solution)/shard_map/pallas_call | solution.py:110
  12.8 1.4 %collective-permute-start.20 = (f32[3,16,1536]{2,1,0:T(8,128)S(1)}, f32[3,16,1536]{2,1,0:T(8,128)S(1)}, u32[]{:S(2)}, u32[]{:S(2)}) collective-permute-start(f32[3,16,1536]{2,1,0:T(8,128)S(1)} %get-tuple-element.36), channel_id=1, source_target_pairs={{0,16},{8,24},{16,0},{24,8},{1,17},{9,25},{17,1},{25,9},{2,18},{10... | collective-permute-start | bytes 884744 | tf_op jit(solution)/shard_map/ppermute | solution.py:132
  14.2 0.7 collective-permute-start.18
  14.9 1.5 %collective-permute-start.5 = (f32[32]{0:T(128)S(1)}, f32[32]{0:T(128)S(1)}, u32[]{:S(2)}, u32[]{:S(2)}) collective-permute-start(f32[32]{0:T(128)S(1)} %add.100), channel_id=1, source_target_pairs={{0,1},{1,0},{2,3},{3,2},{4,5},{5,4},{6,7},{7,6},{8,9},{9,8},{10,11... | collective-permute-start | bytes 392 | tf_op jit(solution)/shard_map/ppermute | solution.py:122
  16.4 1.4 %collective-permute-start.16 = (f32[3,16,1536]{2,1,0:T(8,128)S(1)}, f32[3,16,1536]{2,1,0:T(8,128)S(1)}, u32[]{:S(2)}, u32[]{:S(2)}) collective-permute-start(f32[3,16,1536]{2,1,0:T(8,128)S(1)} %get-tuple-element.32), channel_id=1, source_target_pairs={{0,16},{8,24},{16,0},{24,8},{1,17},{9,25},{17,1},{25,9},{2,18},{10... | collective-permute-start | bytes 884744 | tf_op jit(solution)/shard_map/ppermute | solution.py:132
  17.8 0.7 collective-permute-done.5
  18.5 1.6 %collective-permute-start.6 = (f32[32]{0:T(128)S(1)}, f32[32]{0:T(128)S(1)}, u32[]{:S(2)}, u32[]{:S(2)}) collective-permute-start(f32[32]{0:T(128)S(1)} %add.113), channel_id=1, source_target_pairs={{0,2},{1,3},{2,0},{3,1},{4,6},{5,7},{6,4},{7,5},{8,10},{9,11},{10,... | collective-permute-start | bytes 392 | tf_op jit(solution)/shard_map/ppermute | solution.py:122
  20.1 1.4 %collective-permute-start.14 = (f32[3,16,1536]{2,1,0:T(8,128)S(1)}, f32[3,16,1536]{2,1,0:T(8,128)S(1)}, u32[]{:S(2)}, u32[]{:S(2)}) collective-permute-start(f32[3,16,1536]{2,1,0:T(8,128)S(1)} %get-tuple-element.30), channel_id=1, source_target_pairs={{0,16},{8,24},{16,0},{24,8},{1,17},{9,25},{17,1},{25,9},{2,18},{10... | collective-permute-start | bytes 884744 | tf_op jit(solution)/shard_map/ppermute | solution.py:132
  21.4 0.6 collective-permute-done.6
  22.1 1.4 %collective-permute-start.12 = (f32[3,16,1536]{2,1,0:T(8,128)S(1)}, f32[3,16,1536]{2,1,0:T(8,128)S(1)}, u32[]{:S(2)}, u32[]{:S(2)}) collective-permute-start(f32[3,16,1536]{2,1,0:T(8,128)S(1)} %get-tuple-element.28), channel_id=1, source_target_pairs={{0,16},{8,24},{16,0},{24,8},{1,17},{9,25},{17,1},{25,9},{2,18},{10... | collective-permute-start | bytes 884744 | tf_op jit(solution)/shard_map/ppermute | solution.py:132
  23.4 0.7 fusion.9
  24.1 0.0 collective-permute-done.20.refs_1_
  24.1 0.7 collective-permute-start.10
  24.8 4.3 %collective-permute-done.18.refs_1_ = f32[3,16,1536]{2,1,0:T(8,128)S(1)} collective-permute-done((f32[3,16,1536]{2,1,0:T(8,128)S(1)}, f32[3,16,1536]{2,1,0:T(8,128)S(1)}, u32[]{:S(2)}, u32[]{:S(2)}) %collective-permute-start.18) | collective-permute-done | bytes 294944 | tf_op jit(solution)/shard_map/ppermute | solution.py:132
  29.1 1.4 %collective-permute-start.8 = (f32[3,16,1536]{2,1,0:T(8,128)S(1)}, f32[3,16,1536]{2,1,0:T(8,128)S(1)}, u32[]{:S(2)}, u32[]{:S(2)}) collective-permute-start(f32[3,16,1536]{2,1,0:T(8,128)S(1)} %get-tuple-element.24), channel_id=1, source_target_pairs={{0,16},{8,24},{16,0},{24,8},{1,17},{9,25},{17,1},{25,9},{2,18},{10... | collective-permute-start | bytes 884744 | tf_op jit(solution)/shard_map/ppermute | solution.py:132
  30.4 0.7 shard_map.110
  31.1 0.7 shard_map.109
  31.8 3.6 %collective-permute-done.16.refs_1_ = f32[3,16,1536]{2,1,0:T(8,128)S(1)} collective-permute-done((f32[3,16,1536]{2,1,0:T(8,128)S(1)}, f32[3,16,1536]{2,1,0:T(8,128)S(1)}, u32[]{:S(2)}, u32[]{:S(2)}) %collective-permute-start.16) | collective-permute-done | bytes 294944 | tf_op jit(solution)/shard_map/ppermute | solution.py:132
  35.4 1.4 %collective-permute-start.22 = (f32[3,16,1536]{2,1,0:T(8,128)S(1)}, f32[3,16,1536]{2,1,0:T(8,128)S(1)}, u32[]{:S(2)}, u32[]{:S(2)}) collective-permute-start(f32[3,16,1536]{2,1,0:T(8,128)S(1)} %get-tuple-element.38), channel_id=1, source_target_pairs={{0,16},{8,24},{16,0},{24,8},{1,17},{9,25},{17,1},{25,9},{2,18},{10... | collective-permute-start | bytes 884744 | tf_op jit(solution)/shard_map/ppermute | solution.py:132
  36.8 5.0 %collective-permute-done.14.refs_1_ = f32[3,16,1536]{2,1,0:T(8,128)S(1)} collective-permute-done((f32[3,16,1536]{2,1,0:T(8,128)S(1)}, f32[3,16,1536]{2,1,0:T(8,128)S(1)}, u32[]{:S(2)}, u32[]{:S(2)}) %collective-permute-start.14) | collective-permute-done | bytes 294944 | tf_op jit(solution)/shard_map/ppermute | solution.py:132
  41.7 2.6 %collective-permute-start.21 = (f32[3,16,1536]{2,1,0:T(8,128)S(1)}, f32[3,16,1536]{2,1,0:T(8,128)S(1)}, u32[]{:S(2)}, u32[]{:S(2)}) collective-permute-start(f32[3,16,1536]{2,1,0:T(8,128)S(1)} %shard_map.110), channel_id=1, source_target_pairs={{0,4},{1,5},{2,6},{3,7},{4,0},{5,1},{6,2},{7,3},{8,12},{9,13},{10,... | collective-permute-start | bytes 884744 | tf_op jit(solution)/shard_map/ppermute | solution.py:142
  44.3 3.7 %collective-permute-done.12.refs_1_ = f32[3,16,1536]{2,1,0:T(8,128)S(1)} collective-permute-done((f32[3,16,1536]{2,1,0:T(8,128)S(1)}, f32[3,16,1536]{2,1,0:T(8,128)S(1)}, u32[]{:S(2)}, u32[]{:S(2)}) %collective-permute-start.12) | collective-permute-done | bytes 294944 | tf_op jit(solution)/shard_map/ppermute | solution.py:132
  48.0 3.5 %collective-permute-start.19 = (f32[3,16,1536]{2,1,0:T(8,128)S(1)}, f32[3,16,1536]{2,1,0:T(8,128)S(1)}, u32[]{:S(2)}, u32[]{:S(2)}) collective-permute-start(f32[3,16,1536]{2,1,0:T(8,128)S(1)} %shard_map.109), channel_id=1, source_target_pairs={{0,5},{1,4},{2,7},{3,6},{4,1},{5,0},{6,3},{7,2},{8,13},{9,12},{10,... | collective-permute-start | bytes 884744 | tf_op jit(solution)/shard_map/ppermute | solution.py:142
  51.6 0.7 shard_map.108
  52.3 0.7 shard_map.107
  53.0 0.7 shard_map.106
  53.7 0.7 collective-permute-done.10.refs_1_
  54.4 2.6 %collective-permute-start.7 = (f32[32]{0:T(128)S(1)}, f32[32]{0:T(128)S(1)}, u32[]{:S(2)}, u32[]{:S(2)}) collective-permute-start(f32[32]{0:T(128)S(1)} %add.114), channel_id=1, source_target_pairs={{0,4},{1,5},{2,6},{3,7},{4,0},{5,1},{6,2},{7,3},{8,12},{9,13},{10,... | collective-permute-start | bytes 392 | tf_op jit(solution)/shard_map/ppermute | solution.py:122
  57.0 1.4 %shard_map.105 = f32[3,16,1536]{2,1,0:T(8,128)} custom-call(s32[1]{0:T(128)} %get-tuple-element.45.lag_ref, f32[3,16,1536]{2,1,0:T(8,128)S(1)} %get-tuple-element.25.refs_0_, f32[3,16,1536]{2,1,0:T(8,128)S(1)} %collective-permute-done.10.refs_1_), custom_call_target="tpu_custom_call" | custom-call | tf_op jit(solution)/shard_map/pallas_call | solution.py:133
  58.3 2.4 %collective-permute-done.8.refs_1_ = f32[3,16,1536]{2,1,0:T(8,128)S(1)} collective-permute-done((f32[3,16,1536]{2,1,0:T(8,128)S(1)}, f32[3,16,1536]{2,1,0:T(8,128)S(1)}, u32[]{:S(2)}, u32[]{:S(2)}) %collective-permute-start.8) | collective-permute-done | bytes 294944 | tf_op jit(solution)/shard_map/ppermute | solution.py:132
  60.7 3.6 %collective-permute-start.17 = (f32[3,16,1536]{2,1,0:T(8,128)S(1)}, f32[3,16,1536]{2,1,0:T(8,128)S(1)}, u32[]{:S(2)}, u32[]{:S(2)}) collective-permute-start(f32[3,16,1536]{2,1,0:T(8,128)S(1)} %shard_map.108), channel_id=1, source_target_pairs={{0,6},{1,7},{2,4},{3,5},{4,2},{5,3},{6,0},{7,1},{8,14},{9,15},{10,... | collective-permute-start | bytes 884744 | tf_op jit(solution)/shard_map/ppermute | solution.py:142
  64.3 1.4 %shard_map.104 = f32[3,16,1536]{2,1,0:T(8,128)} custom-call(s32[1]{0:T(128)} %get-tuple-element.46.lag_ref, f32[3,16,1536]{2,1,0:T(8,128)S(1)} %get-tuple-element.23.refs_0_, f32[3,16,1536]{2,1,0:T(8,128)S(1)} %collective-permute-done.8.refs_1_), custom_call_target="tpu_custom_call" | custom-call | tf_op jit(solution)/shard_map/pallas_call | solution.py:133
  65.7 10.7 %collective-permute-done.7 = f32[32]{0:T(128)S(1)} collective-permute-done((f32[32]{0:T(128)S(1)}, f32[32]{0:T(128)S(1)}, u32[]{:S(2)}, u32[]{:S(2)}) %collective-permute-start.7) | collective-permute-done | bytes 160 | tf_op jit(solution)/shard_map/ppermute | solution.py:122
  76.5 3.4 %collective-permute-start.15 = (f32[3,16,1536]{2,1,0:T(8,128)S(1)}, f32[3,16,1536]{2,1,0:T(8,128)S(1)}, u32[]{:S(2)}, u32[]{:S(2)}) collective-permute-start(f32[3,16,1536]{2,1,0:T(8,128)S(1)} %shard_map.107), channel_id=1, source_target_pairs={{0,7},{1,6},{2,5},{3,4},{4,3},{5,2},{6,1},{7,0},{8,15},{9,14},{10,... | collective-permute-start | bytes 884744 | tf_op jit(solution)/shard_map/ppermute | solution.py:142
  79.9 0.0 collective-permute-start.13
  79.9 0.0 collective-permute-done.21.refs_6_
  79.9 2.0 %collective-permute-start.11 = (f32[3,16,1536]{2,1,0:T(8,128)}, f32[3,16,1536]{2,1,0:T(8,128)S(1)}, u32[]{:S(2)}, u32[]{:S(2)}) collective-permute-start(f32[3,16,1536]{2,1,0:T(8,128)} %shard_map.105), channel_id=1, source_target_pairs={{0,2},{1,3},{2,0},{3,1},{4,6},{5,7},{6,4},{7,5},{8,10},{9,11},{10,... | collective-permute-start | bytes 884744 | tf_op jit(solution)/shard_map/ppermute | solution.py:142
  81.9 1.5 %collective-permute-start.9 = (f32[3,16,1536]{2,1,0:T(8,128)}, f32[3,16,1536]{2,1,0:T(8,128)S(1)}, u32[]{:S(2)}, u32[]{:S(2)}) collective-permute-start(f32[3,16,1536]{2,1,0:T(8,128)} %shard_map.104), channel_id=1, source_target_pairs={{0,1},{1,0},{2,3},{3,2},{4,5},{5,4},{6,7},{7,6},{8,9},{9,8},{10,11... | collective-permute-start | bytes 884744 | tf_op jit(solution)/shard_map/ppermute | solution.py:142
  83.4 0.7 fusion.1
  84.0 0.7 shard_map.111.refs_7_
  84.8 4.3 %collective-permute-done.15.refs_3_ = f32[3,16,1536]{2,1,0:T(8,128)S(1)} collective-permute-done((f32[3,16,1536]{2,1,0:T(8,128)S(1)}, f32[3,16,1536]{2,1,0:T(8,128)S(1)}, u32[]{:S(2)}, u32[]{:S(2)}) %collective-permute-start.15) | collective-permute-done | bytes 294944 | tf_op jit(solution)/shard_map/ppermute | solution.py:142
  89.1 7.8 %collective-permute-done.13.refs_2_ = f32[3,16,1536]{2,1,0:T(8,128)S(1)} collective-permute-done((f32[3,16,1536]{2,1,0:T(8,128)S(1)}, f32[3,16,1536]{2,1,0:T(8,128)S(1)}, u32[]{:S(2)}, u32[]{:S(2)}) %collective-permute-start.13) | collective-permute-done | bytes 294944 | tf_op jit(solution)/shard_map/ppermute | solution.py:142
  96.9 5.4 %collective-permute-done.11.refs_1_ = f32[3,16,1536]{2,1,0:T(8,128)S(1)} collective-permute-done((f32[3,16,1536]{2,1,0:T(8,128)}, f32[3,16,1536]{2,1,0:T(8,128)S(1)}, u32[]{:S(2)}, u32[]{:S(2)}) %collective-permute-start.11) | collective-permute-done | bytes 294944 | tf_op jit(solution)/shard_map/ppermute | solution.py:142
  102.4 3.4 %shard_map.112 = (f32[1,128,1536]{2,1,0:T(8,128)}, f32[1,128,1536]{2,1,0:T(8,128)}, f32[1,128,1536]{2,1,0:T(8,128)}) custom-call(s32[8]{0:T(128)S(1)} %broadcast_xor_fusion.place_ref, f32[1]{0:T(128)} %bitcast.1.count_ref, bf16[1,128,1536]{2,1,0:T(8,128)(2,1)S(1)} %copy-done.3, f32[3,16,1536]{2,1,0:T(8,128)S(1)} %collective-permute-done.9.refs_0_, ...), custom_call_target="tpu_custom_call" | custom-call | tf_op jit(solution)/shard_map/pallas_call | solution.py:147
  (23 shorter events, 0.1 us)
Async XLA Ops:
  0.6 7.7 %collective-permute-start.2 = (f32[8,16,1536]{2,1,0:T(8,128)}, f32[8,16,1536]{2,1,0:T(8,128)S(1)}, u32[]{:S(2)}, u32[]{:S(2)}) collective-permute-start(f32[8,16,1536]{2,1,0:T(8,128)} %refs_0_.1), channel_id=1, source_target_pairs={{0,8},{8,0},{16,24},{24,16},{1,9},{9,1},{17,25},{25,17},{2,10},{10... | collective-permute-start | bytes 2359304 | tf_op jit(solution)/shard_map/ppermute | solution.py:88
  1.2 7.1 %collective-permute-start.3 = (f32[8,16,1536]{2,1,0:T(8,128)}, f32[8,16,1536]{2,1,0:T(8,128)S(1)}, u32[]{:S(2)}, u32[]{:S(2)}) collective-permute-start(f32[8,16,1536]{2,1,0:T(8,128)} %refs_1_.1), channel_id=1, source_target_pairs={{0,8},{8,0},{16,24},{24,16},{1,9},{9,1},{17,25},{25,17},{2,10},{10... | collective-permute-start | bytes 2359304 | tf_op jit(solution)/shard_map/ppermute | solution.py:88
  1.3 7.1 %collective-permute-start.4 = (f32[8,16,1536]{2,1,0:T(8,128)}, f32[8,16,1536]{2,1,0:T(8,128)S(1)}, u32[]{:S(2)}, u32[]{:S(2)}) collective-permute-start(f32[8,16,1536]{2,1,0:T(8,128)} %refs_2_.1), channel_id=1, source_target_pairs={{0,8},{8,0},{16,24},{24,16},{1,9},{9,1},{17,25},{25,17},{2,10},{10... | collective-permute-start | bytes 2359304 | tf_op jit(solution)/shard_map/ppermute | solution.py:88
  2.4 4.2 %collective-permute-start = (f32[32]{0:T(128)S(1)}, f32[32]{0:T(128)S(1)}, u32[]{:S(2)}, u32[]{:S(2)}) collective-permute-start(f32[32]{0:T(128)S(1)} %convert_bitcast_fusion), channel_id=1, source_target_pairs={{0,16},{8,24},{16,0},{24,8},{1,17},{9,25},{17,1},{25,9},{2,18},{10... | collective-permute-start | bytes 392 | tf_op jit(solution)/shard_map/ppermute | solution.py:105
  4.9 0.7 copy-start.7
  5.6 0.7 copy-start.4
  5.6 0.7 copy-start.5
  6.5 0.7 copy-start.6
  7.2 1.2 %collective-permute-start.1 = (f32[32]{0:T(128)S(1)}, f32[32]{0:T(128)S(1)}, u32[]{:S(2)}, u32[]{:S(2)}) collective-permute-start(f32[32]{0:T(128)S(1)} %fusion.8), channel_id=1, source_target_pairs={{0,8},{8,0},{16,24},{24,16},{1,9},{9,1},{17,25},{25,17},{2,10},{10... | collective-permute-start | bytes 392 | tf_op jit(solution)/shard_map/ppermute | solution.py:107
  8.3 1.1 %copy-start = (f32[8,16,1536]{2,1,0:T(8,128)S(1)}, f32[8,16,1536]{2,1,0:T(8,128)}, u32[]{:S(2)}) copy-start(f32[8,16,1536]{2,1,0:T(8,128)} %refs_0_.1) | copy-start | bytes 2359300
  9.5 1.1 %copy-start.1 = (f32[8,16,1536]{2,1,0:T(8,128)S(1)}, f32[8,16,1536]{2,1,0:T(8,128)}, u32[]{:S(2)}) copy-start(f32[8,16,1536]{2,1,0:T(8,128)} %refs_1_.1) | copy-start | bytes 2359300
  10.6 1.1 %copy-start.2 = (f32[8,16,1536]{2,1,0:T(8,128)S(1)}, f32[8,16,1536]{2,1,0:T(8,128)}, u32[]{:S(2)}) copy-start(f32[8,16,1536]{2,1,0:T(8,128)} %refs_2_.1) | copy-start | bytes 2359300
  12.8 11.3 %collective-permute-start.20 = (f32[3,16,1536]{2,1,0:T(8,128)S(1)}, f32[3,16,1536]{2,1,0:T(8,128)S(1)}, u32[]{:S(2)}, u32[]{:S(2)}) collective-permute-start(f32[3,16,1536]{2,1,0:T(8,128)S(1)} %get-tuple-element.36), channel_id=1, source_target_pairs={{0,16},{8,24},{16,0},{24,8},{1,17},{9,25},{17,1},{25,9},{2,18},{10... | collective-permute-start | bytes 884744 | tf_op jit(solution)/shard_map/ppermute | solution.py:132
  14.2 14.8 %collective-permute-start.18 = (f32[3,16,1536]{2,1,0:T(8,128)S(1)}, f32[3,16,1536]{2,1,0:T(8,128)S(1)}, u32[]{:S(2)}, u32[]{:S(2)}) collective-permute-start(f32[3,16,1536]{2,1,0:T(8,128)S(1)} %get-tuple-element.34), channel_id=1, source_target_pairs={{0,16},{8,24},{16,0},{24,8},{1,17},{9,25},{17,1},{25,9},{2,18},{10... | collective-permute-start | bytes 884744 | tf_op jit(solution)/shard_map/ppermute | solution.py:132
  14.9 3.6 %collective-permute-start.5 = (f32[32]{0:T(128)S(1)}, f32[32]{0:T(128)S(1)}, u32[]{:S(2)}, u32[]{:S(2)}) collective-permute-start(f32[32]{0:T(128)S(1)} %add.100), channel_id=1, source_target_pairs={{0,1},{1,0},{2,3},{3,2},{4,5},{5,4},{6,7},{7,6},{8,9},{9,8},{10,11... | collective-permute-start | bytes 392 | tf_op jit(solution)/shard_map/ppermute | solution.py:122
  16.4 19.0 %collective-permute-start.16 = (f32[3,16,1536]{2,1,0:T(8,128)S(1)}, f32[3,16,1536]{2,1,0:T(8,128)S(1)}, u32[]{:S(2)}, u32[]{:S(2)}) collective-permute-start(f32[3,16,1536]{2,1,0:T(8,128)S(1)} %get-tuple-element.32), channel_id=1, source_target_pairs={{0,16},{8,24},{16,0},{24,8},{1,17},{9,25},{17,1},{25,9},{2,18},{10... | collective-permute-start | bytes 884744 | tf_op jit(solution)/shard_map/ppermute | solution.py:132
  18.5 3.6 %collective-permute-start.6 = (f32[32]{0:T(128)S(1)}, f32[32]{0:T(128)S(1)}, u32[]{:S(2)}, u32[]{:S(2)}) collective-permute-start(f32[32]{0:T(128)S(1)} %add.113), channel_id=1, source_target_pairs={{0,2},{1,3},{2,0},{3,1},{4,6},{5,7},{6,4},{7,5},{8,10},{9,11},{10,... | collective-permute-start | bytes 392 | tf_op jit(solution)/shard_map/ppermute | solution.py:122
  20.1 21.7 %collective-permute-start.14 = (f32[3,16,1536]{2,1,0:T(8,128)S(1)}, f32[3,16,1536]{2,1,0:T(8,128)S(1)}, u32[]{:S(2)}, u32[]{:S(2)}) collective-permute-start(f32[3,16,1536]{2,1,0:T(8,128)S(1)} %get-tuple-element.30), channel_id=1, source_target_pairs={{0,16},{8,24},{16,0},{24,8},{1,17},{9,25},{17,1},{25,9},{2,18},{10... | collective-permute-start | bytes 884744 | tf_op jit(solution)/shard_map/ppermute | solution.py:132
  22.1 26.0 %collective-permute-start.12 = (f32[3,16,1536]{2,1,0:T(8,128)S(1)}, f32[3,16,1536]{2,1,0:T(8,128)S(1)}, u32[]{:S(2)}, u32[]{:S(2)}) collective-permute-start(f32[3,16,1536]{2,1,0:T(8,128)S(1)} %get-tuple-element.28), channel_id=1, source_target_pairs={{0,16},{8,24},{16,0},{24,8},{1,17},{9,25},{17,1},{25,9},{2,18},{10... | collective-permute-start | bytes 884744 | tf_op jit(solution)/shard_map/ppermute | solution.py:132
  24.1 30.2 %collective-permute-start.10 = (f32[3,16,1536]{2,1,0:T(8,128)S(1)}, f32[3,16,1536]{2,1,0:T(8,128)S(1)}, u32[]{:S(2)}, u32[]{:S(2)}) collective-permute-start(f32[3,16,1536]{2,1,0:T(8,128)S(1)} %get-tuple-element.26), channel_id=1, source_target_pairs={{0,16},{8,24},{16,0},{24,8},{1,17},{9,25},{17,1},{25,9},{2,18},{10... | collective-permute-start | bytes 884744 | tf_op jit(solution)/shard_map/ppermute | solution.py:132
  29.1 31.6 %collective-permute-start.8 = (f32[3,16,1536]{2,1,0:T(8,128)S(1)}, f32[3,16,1536]{2,1,0:T(8,128)S(1)}, u32[]{:S(2)}, u32[]{:S(2)}) collective-permute-start(f32[3,16,1536]{2,1,0:T(8,128)S(1)} %get-tuple-element.24), channel_id=1, source_target_pairs={{0,16},{8,24},{16,0},{24,8},{1,17},{9,25},{17,1},{25,9},{2,18},{10... | collective-permute-start | bytes 884744 | tf_op jit(solution)/shard_map/ppermute | solution.py:132
  35.4 44.5 %collective-permute-start.22 = (f32[3,16,1536]{2,1,0:T(8,128)S(1)}, f32[3,16,1536]{2,1,0:T(8,128)S(1)}, u32[]{:S(2)}, u32[]{:S(2)}) collective-permute-start(f32[3,16,1536]{2,1,0:T(8,128)S(1)} %get-tuple-element.38), channel_id=1, source_target_pairs={{0,16},{8,24},{16,0},{24,8},{1,17},{9,25},{17,1},{25,9},{2,18},{10... | collective-permute-start | bytes 884744 | tf_op jit(solution)/shard_map/ppermute | solution.py:132
  41.7 38.1 %collective-permute-start.21 = (f32[3,16,1536]{2,1,0:T(8,128)S(1)}, f32[3,16,1536]{2,1,0:T(8,128)S(1)}, u32[]{:S(2)}, u32[]{:S(2)}) collective-permute-start(f32[3,16,1536]{2,1,0:T(8,128)S(1)} %shard_map.110), channel_id=1, source_target_pairs={{0,4},{1,5},{2,6},{3,7},{4,0},{5,1},{6,2},{7,3},{8,12},{9,13},{10,... | collective-permute-start | bytes 884744 | tf_op jit(solution)/shard_map/ppermute | solution.py:142
  48.0 33.8 %collective-permute-start.19 = (f32[3,16,1536]{2,1,0:T(8,128)S(1)}, f32[3,16,1536]{2,1,0:T(8,128)S(1)}, u32[]{:S(2)}, u32[]{:S(2)}) collective-permute-start(f32[3,16,1536]{2,1,0:T(8,128)S(1)} %shard_map.109), channel_id=1, source_target_pairs={{0,5},{1,4},{2,7},{3,6},{4,1},{5,0},{6,3},{7,2},{8,13},{9,12},{10,... | collective-permute-start | bytes 884744 | tf_op jit(solution)/shard_map/ppermute | solution.py:142
  54.4 22.1 %collective-permute-start.7 = (f32[32]{0:T(128)S(1)}, f32[32]{0:T(128)S(1)}, u32[]{:S(2)}, u32[]{:S(2)}) collective-permute-start(f32[32]{0:T(128)S(1)} %add.114), channel_id=1, source_target_pairs={{0,4},{1,5},{2,6},{3,7},{4,0},{5,1},{6,2},{7,3},{8,12},{9,13},{10,... | collective-permute-start | bytes 392 | tf_op jit(solution)/shard_map/ppermute | solution.py:122
  60.7 24.1 %collective-permute-start.17 = (f32[3,16,1536]{2,1,0:T(8,128)S(1)}, f32[3,16,1536]{2,1,0:T(8,128)S(1)}, u32[]{:S(2)}, u32[]{:S(2)}) collective-permute-start(f32[3,16,1536]{2,1,0:T(8,128)S(1)} %shard_map.108), channel_id=1, source_target_pairs={{0,6},{1,7},{2,4},{3,5},{4,2},{5,3},{6,0},{7,1},{8,14},{9,15},{10,... | collective-permute-start | bytes 884744 | tf_op jit(solution)/shard_map/ppermute | solution.py:142
  76.5 12.6 %collective-permute-start.15 = (f32[3,16,1536]{2,1,0:T(8,128)S(1)}, f32[3,16,1536]{2,1,0:T(8,128)S(1)}, u32[]{:S(2)}, u32[]{:S(2)}) collective-permute-start(f32[3,16,1536]{2,1,0:T(8,128)S(1)} %shard_map.107), channel_id=1, source_target_pairs={{0,7},{1,6},{2,5},{3,4},{4,3},{5,2},{6,1},{7,0},{8,15},{9,14},{10,... | collective-permute-start | bytes 884744 | tf_op jit(solution)/shard_map/ppermute | solution.py:142
  79.9 17.1 %collective-permute-start.13 = (f32[3,16,1536]{2,1,0:T(8,128)S(1)}, f32[3,16,1536]{2,1,0:T(8,128)S(1)}, u32[]{:S(2)}, u32[]{:S(2)}) collective-permute-start(f32[3,16,1536]{2,1,0:T(8,128)S(1)} %shard_map.106), channel_id=1, source_target_pairs={{0,3},{1,2},{2,1},{3,0},{4,7},{5,6},{6,5},{7,4},{8,11},{9,10},{10,... | collective-permute-start | bytes 884744 | tf_op jit(solution)/shard_map/ppermute | solution.py:142
  79.9 22.5 %collective-permute-start.11 = (f32[3,16,1536]{2,1,0:T(8,128)}, f32[3,16,1536]{2,1,0:T(8,128)S(1)}, u32[]{:S(2)}, u32[]{:S(2)}) collective-permute-start(f32[3,16,1536]{2,1,0:T(8,128)} %shard_map.105), channel_id=1, source_target_pairs={{0,2},{1,3},{2,0},{3,1},{4,6},{5,7},{6,4},{7,5},{8,10},{9,11},{10,... | collective-permute-start | bytes 884744 | tf_op jit(solution)/shard_map/ppermute | solution.py:142
  81.9 20.5 %collective-permute-start.9 = (f32[3,16,1536]{2,1,0:T(8,128)}, f32[3,16,1536]{2,1,0:T(8,128)S(1)}, u32[]{:S(2)}, u32[]{:S(2)}) collective-permute-start(f32[3,16,1536]{2,1,0:T(8,128)} %shard_map.104), channel_id=1, source_target_pairs={{0,1},{1,0},{2,3},{3,2},{4,5},{5,4},{6,7},{7,6},{8,9},{9,8},{10,11... | collective-permute-start | bytes 884744 | tf_op jit(solution)/shard_map/ppermute | solution.py:142
  84.0 18.3 %copy-start.3 = (bf16[1,128,1536]{2,1,0:T(8,128)(2,1)S(1)}, bf16[1,128,1536]{2,1,0:T(8,128)(2,1)}, u32[]{:S(2)}) copy-start(bf16[1,128,1536]{2,1,0:T(8,128)(2,1)} %grad_ref.1) | copy-start | bytes 1179652
